TPU v7x, 32 devices: a whole 2x2x4 slice. The times are simulated.
32 devices in a mesh: row: 8 (over y, x, core), col: 4 (over z).
Axes of the slice: x: 2, y: 2, z: 4, core: 2. Of those that a mesh axis runs over, the one named last changes fastest.
Arguments:
- object_slices: float32 [2, 2, 1024, 512], P(None, None, 'row', 'col'), may hold values from -5 to 5
- probe: float32 [2, 256, 256], replicated, may hold values from -6 to 6
- offsets: int32 [8, 4, 1, 2], P('row', 'col'), may hold values from 0 to 127
- residuals: float32 [8, 4, 1, 2, 256, 256], P('row', 'col'), may hold values from -6 to 6
Outputs:
- new_object: float32 [2, 2, 1024, 512], P(None, None, 'row', 'col')
All inputs are finite; a program needn't handle non-finite values.
Results may differ from a plain program's by a relative error of at most 0.0003.
Values sent between devices are 32-bit elements; how exact they have to be, the bound alone decides.
No kernel may reach another device: no remote copies, remote signals or barrier semaphores. Data moves between devices by JAX's collectives and lax.ppermute only.
A program may use at most 64 MiB of HBM per device.

v0:
```python
from functools import partial
import math

import jax
import jax.numpy as jnp
from jax import lax
from jax.sharding import PartitionSpec as P

FRESNEL = 40.0
STEP_SIZE = 0.5
REGULAR = 1.0


def passed_along(value, axis, steps):
    count = lax.axis_size(axis)
    pairs = [(source, (source + steps) % count) for source in range(count)]
    return lax.ppermute(value, axis, pairs)


def complex_dot(left_re, left_im, right_re, right_im):
    matmul = partial(jnp.dot, precision=lax.Precision.HIGHEST, preferred_element_type=jnp.float32)
    return (
        matmul(left_re, right_re) - matmul(left_im, right_im),
        matmul(left_re, right_im) + matmul(left_im, right_re),
    )


def sandwich(mat_re, mat_im, wave_re, wave_im):
    inner_re, inner_im = complex_dot(mat_re, mat_im, wave_re, wave_im)
    return complex_dot(inner_re, inner_im, mat_re, mat_im)


def tables(width):
    index = jnp.arange(width, dtype=jnp.int32)
    product = index[:, None] * index[None, :] % width
    angle = 2.0 * math.pi / width * product.astype(jnp.float32)
    factor = 1.0 / math.sqrt(width)
    four_re = jnp.cos(angle) * factor
    four_im = -jnp.sin(angle) * factor
    freq = jnp.where(index < width // 2, index, index - width).astype(jnp.float32) / width
    phase = FRESNEL * math.pi * freq * freq
    kern_re = jnp.cos(phase)
    kern_im = -jnp.sin(phase)
    scaled_re = four_re * kern_re[None, :] + four_im * kern_im[None, :]
    scaled_im = four_re * kern_im[None, :] - four_im * kern_re[None, :]
    prop_re, prop_im = complex_dot(scaled_re, scaled_im, four_re, four_im)
    return (four_re, four_im, prop_re, prop_im)


def one_position(window, probe, resid, four_re, four_im, prop_re, prop_im):
    layers = window.shape[0]
    wave_re, wave_im = (probe[0], probe[1])
    waves = [(wave_re, wave_im)]
    layer = 0
    trans_re = window[layer, 0]
    trans_im = window[layer, 1]
    exit_re = wave_re * trans_re - wave_im * trans_im
    exit_im = wave_re * trans_im + wave_im * trans_re
    wave_re, wave_im = sandwich(prop_re, prop_im, exit_re, exit_im)
    waves.append((wave_re, wave_im))
    back_re, back_im = sandwich(four_re, -four_im, resid[0], resid[1])
    parts = [None] * layers
    for layer in reversed(range(layers)):
        wave_re, wave_im = waves[layer]
        parts[layer] = jnp.stack(
            [
                wave_re * back_re + wave_im * back_im,
                wave_re * back_im - wave_im * back_re,
                wave_re * wave_re + wave_im * wave_im,
            ]
        )
        if layer > 0:
            trans_re, trans_im = (window[layer, 0], window[layer, 1])
            pulled_re = trans_re * back_re + trans_im * back_im
            pulled_im = trans_re * back_im - trans_im * back_re
            back_re, back_im = sandwich(prop_re, -prop_im, pulled_re, pulled_im)
    return jnp.stack(parts)


def rows_pass(buffer):
    third = buffer.shape[2] // 3
    strips = [buffer[:, :, band * third : (band + 1) * third] for band in range(3)]
    total = strips[2]
    for band in (1, 0):
        total = passed_along(total, "row", 1) + strips[band]
    return total


def cols_pass(buffer):
    third = buffer.shape[3] // 3
    strips = [buffer[:, :, :, band * third : (band + 1) * third] for band in range(3)]
    total = strips[2]
    for band in (1, 0):
        total = passed_along(total, "col", 1) + strips[band]
    return total


def build_region(object_slices):
    pieces = [object_slices]
    current = object_slices
    for band in range(2):
        current = passed_along(current, "row", -1)
        pieces.append(current)
    column = jnp.concatenate(pieces, axis=2)
    pieces = [column]
    current = column
    for band in range(2):
        current = passed_along(current, "col", -1)
        pieces.append(current)
    return jnp.concatenate(pieces, axis=3)


def local(object_slices, probe, offsets, residuals):
    layers = object_slices.shape[0]
    width = probe.shape[1]
    region = build_region(object_slices)
    four_re, four_im, prop_re, prop_im = tables(width)
    buffer = jnp.zeros((layers, 3, region.shape[2], region.shape[3]), jnp.float32)
    zero = jnp.zeros((), jnp.int32)
    top = offsets[0, 0, 0, 0]
    left = offsets[0, 0, 0, 1]
    window = lax.dynamic_slice(region, (zero, zero, top, left), (layers, 2, width, width))
    contrib = one_position(window, probe, residuals[0, 0, 0], four_re, four_im, prop_re, prop_im)
    older = lax.dynamic_slice(buffer, (zero, zero, top, left), (layers, 3, width, width))
    buffer = lax.dynamic_update_slice(buffer, older + contrib, (zero, zero, top, left))
    gathered = cols_pass(rows_pass(buffer))
    gradient = gathered[:, 0:2]
    illumination = gathered[:, 2:3]
    return object_slices - STEP_SIZE * gradient / (illumination + REGULAR)


def solution(mesh):
    placed = (
        P(None, None, "row", "col"),
        P(),
        P("row", "col", None, None),
        P("row", "col", None, None, None, None),
    )
    return jax.shard_map(
        local, mesh=mesh, in_specs=placed, out_specs=P(None, None, "row", "col"), check_vma=False
    )
```

profile of v0, /device:TPU:0, one launch (start us, length us, event | category | flops | bytes accessed | tf_op | source)
XLA Modules:
  0.0 143.5 jit_solution(12569929631615986170)
XLA Ops:
  0.0 3.4 %collective-permute-start = (f32[2,2,128,128]{3,2,1,0:T(8,128)}, f32[2,2,128,128]{3,2,1,0:T(8,128)S(1)}, u32[]{:S(2)}, u32[]{:S(2)}) collective-permute-start(f32[2,2,128,128]{3,2,1,0:T(8,128)} %param.4), channel_id=1, source_target_pairs={{0,28},{4,0},{8,4},{12,8},{16,12},{20,16},{24,20},{28,24},{1,29},{... | collective-permute-start | bytes 786440 | tf_op jit(solution)/shard_map/ppermute | solution.py:17
  3.4 3.0 %fusion.13 = f32[256,256]{1,0:T(8,128)} fusion(f32[1,1,1,2,256,256]{5,4,3,2,1,0:T(8,128)} %param.7), kind=kOutput, calls=%fused_computation.49 | convolution fusion | flops 202309632 | bytes 524288 | tf_op jit(solution)/shard_map/dot_general | solution.py:24
  6.4 1.4 fusion.17
  7.8 1.4 convolution_subtract_fusion.5
  9.2 2.1 %fusion.42 = f32[256,256]{1,0:T(8,128)} fusion(f32[256,256]{1,0:T(8,128)S(1)} %convolution_subtract_fusion.5), kind=kOutput, calls=%fused_computation.92 | convolution fusion | flops 202440704 | bytes 524288 | tf_op jit(solution)/shard_map/dot_general | solution.py:24
  11.3 0.7 collective-permute-start.1
  11.9 1.5 %fusion.26 = f32[256,256]{1,0:T(8,128)S(1)} fusion(f32[256]{0:T(256)S(1)} %get-tuple-element.19, f32[256]{0:T(256)S(1)} %get-tuple-element.20), kind=kOutput, calls=%fused_computation.75 | convolution fusion | flops 203554816 | bytes 264192 | tf_op jit(solution)/shard_map/dot_general | solution.py:24
  13.5 2.4 %collective-permute-done.1 = f32[2,2,128,128]{3,2,1,0:T(8,128)S(1)} collective-permute-done((f32[2,2,128,128]{3,2,1,0:T(8,128)S(1)}, f32[2,2,128,128]{3,2,1,0:T(8,128)S(1)}, u32[]{:S(2)}, u32[]{:S(2)}) %collective-permute-start.1) | collective-permute-done | bytes 262176 | tf_op jit(solution)/shard_map/ppermute | solution.py:17
  15.8 3.8 %collective-permute-start.2 = (f32[2,2,384,128]{3,2,1,0:T(8,128)S(1)}, f32[2,2,384,128]{3,2,1,0:T(8,128)S(1)}, u32[]{:S(2)}, u32[]{:S(2)}) collective-permute-start(f32[2,2,384,128]{3,2,1,0:T(8,128)S(1)} %constant_dynamic-update-slice_fusion), channel_id=1, source_target_pairs={{0,3},{1,0},{2,1},{3,2},{4,7},{5,4},{6,5},{7,6},{8,11},{9,8},{10,9... | collective-permute-start | bytes 2359304 | tf_op jit(solution)/shard_map/ppermute | solution.py:17
  19.7 2.2 %fusion.40 = f32[256,256]{1,0:T(8,128)} fusion(f32[256]{0:T(256)S(1)} %get-tuple-element.19, f32[256]{0:T(256)S(1)} %get-tuple-element.20), kind=kOutput, calls=%fused_computation.90 | convolution fusion | flops 203489280 | bytes 264192 | tf_op jit(solution)/shard_map/dot_general | solution.py:23
  21.8 2.1 %fusion.37 = f32[256,256]{1,0:T(8,128)} fusion(f32[256,256]{1,0:T(8,128)S(1)} %convolution_subtract_fusion.5), kind=kOutput, calls=%fused_computation.87 | convolution fusion | flops 202309632 | bytes 524288 | tf_op jit(solution)/shard_map/dot_general | solution.py:23
  24.0 1.5 %convolution_add_fusion.4 = f32[256,256]{1,0:T(8,128)S(1)} fusion(f32[256,256]{1,0:T(8,128)S(1)} %fusion.26, f32[256]{0:T(256)S(1)} %get-tuple-element.19, f32[256]{0:T(256)S(1)} %get-tuple-element.20), kind=kOutput, calls=%fused_computation.14 | convolution fusion | flops 203554816 | bytes 526336 | tf_op jit(solution)/shard_map/dot_general | solution.py:24
  25.4 11.1 %collective-permute-done.2 = f32[2,2,384,128]{3,2,1,0:T(8,128)S(1)} collective-permute-done((f32[2,2,384,128]{3,2,1,0:T(8,128)S(1)}, f32[2,2,384,128]{3,2,1,0:T(8,128)S(1)}, u32[]{:S(2)}, u32[]{:S(2)}) %collective-permute-start.2) | collective-permute-done | bytes 786464 | tf_op jit(solution)/shard_map/ppermute | solution.py:17
  36.5 4.3 %collective-permute-start.3 = (f32[2,2,384,128]{3,2,1,0:T(8,128)S(1)}, f32[2,2,384,128]{3,2,1,0:T(8,128)S(1)}, u32[]{:S(2)}, u32[]{:S(2)}) collective-permute-start(f32[2,2,384,128]{3,2,1,0:T(8,128)S(1)} %collective-permute-done.2), channel_id=1, source_target_pairs={{0,3},{1,0},{2,1},{3,2},{4,7},{5,4},{6,5},{7,6},{8,11},{9,8},{10,9... | collective-permute-start | bytes 2359304 | tf_op jit(solution)/shard_map/ppermute | solution.py:17
  40.8 0.6 fusion.130
  45.2 2.5 %convolution_subtract_fusion.6 = f32[256,256]{1,0:T(8,128)S(1)} fusion(f32[256,256]{1,0:T(8,128)} %fusion.40, f32[256]{0:T(256)S(1)} %get-tuple-element.19, f32[256]{0:T(256)S(1)} %get-tuple-element.20), kind=kOutput, calls=%fused_computation.19 | convolution fusion | flops 203620352 | bytes 526336 | tf_op jit(solution)/shard_map/dot_general | solution.py:23
  47.7 1.4 convolution_add_fusion.6
  49.1 1.4 convolution_add_fusion.5
  50.5 6.2 %collective-permute-done.3 = f32[2,2,384,128]{3,2,1,0:T(8,128)S(1)} collective-permute-done((f32[2,2,384,128]{3,2,1,0:T(8,128)S(1)}, f32[2,2,384,128]{3,2,1,0:T(8,128)S(1)}, u32[]{:S(2)}, u32[]{:S(2)}) %collective-permute-start.3) | collective-permute-done | bytes 786464 | tf_op jit(solution)/shard_map/ppermute | solution.py:17
  56.7 0.8 fusion.1
  57.5 1.4 multiply_subtract_fusion
  59.0 0.4 fusion.135
  59.4 0.4 fusion.133
  59.7 0.4 convolution_subtract_fusion.3
  60.1 0.4 fusion.29
  60.5 0.4 fusion.134
  60.9 0.4 fusion.136
  61.3 0.4 fusion.138
  61.7 0.4 convolution_subtract_fusion.1
  62.1 0.4 fusion.139
  62.5 0.4 fusion.137
  62.9 0.4 convolution_add_fusion.3
  63.2 0.4 convolution_add_fusion.1
  63.6 0.4 convolution_add_fusion
  64.0 0.4 convolution_subtract_fusion
  64.4 0.6 convolution_add_fusion.2
  65.0 0.4 fusion.8
  65.7 1.3 pad_maximum_fusion
  66.9 0.2 broadcast_in_dim.2
  67.2 20.5 %dynamic_update_slice.3 = f32[2,3,384,384]{3,2,1,0:T(8,128)S(1)} dynamic-update-slice(f32[2,3,384,384]{3,2,1,0:T(8,128)S(1)} %broadcast_in_dim.2, f32[2,3,256,256]{3,2,1,0:T(8,128)} %pad_maximum_fusion, s32[]{:T(128)} %constant.14.clone.1, s32[]{:T(128)} %constant.14.clone.1, s32[]{:T(128)S(6)} %select_n.64, s32[]{:T(128)S(6)} %select_n.65) | dynamic-update-slice | bytes 3145732 | tf_op jit(solution)/shard_map/dynamic_update_slice | solution.py:125
  87.9 17.2 %collective-permute-done.4 = f32[2,3,128,384]{3,2,1,0:T(8,128)S(1)} collective-permute-done((f32[2,3,128,384]{3,2,1,0:T(8,128)S(1)}, f32[2,3,128,384]{3,2,1,0:T(8,128)S(1)}, u32[]{:S(2)}, u32[]{:S(2)}) %collective-permute-start.4) | collective-permute-done | bytes 1179680 | tf_op jit(solution)/shard_map/ppermute | solution.py:17
  105.1 0.2 slice_add_fusion.1
  105.4 16.5 %collective-permute-done.5 = f32[2,3,128,384]{3,2,1,0:T(8,128)S(1)} collective-permute-done((f32[2,3,128,384]{3,2,1,0:T(8,128)S(1)}, f32[2,3,128,384]{3,2,1,0:T(8,128)S(1)}, u32[]{:S(2)}, u32[]{:S(2)}) %collective-permute-start.5) | collective-permute-done | bytes 1179680 | tf_op jit(solution)/shard_map/ppermute | solution.py:17
  121.9 0.2 slice_add_fusion
  122.2 10.1 %collective-permute-done.6 = f32[2,3,128,128]{3,2,1,0:T(8,128)S(1)} collective-permute-done((f32[2,3,128,128]{3,2,1,0:T(8,128)S(1)}, f32[2,3,128,128]{3,2,1,0:T(8,128)S(1)}, u32[]{:S(2)}, u32[]{:S(2)}) %collective-permute-start.6) | collective-permute-done | bytes 393248 | tf_op jit(solution)/shard_map/ppermute | solution.py:17
  132.4 0.5 collective-permute-start.7
  132.8 9.9 %collective-permute-done.7 = f32[2,3,128,128]{3,2,1,0:T(8,128)S(1)} collective-permute-done((f32[2,3,128,128]{3,2,1,0:T(8,128)S(1)}, f32[2,3,128,128]{3,2,1,0:T(8,128)S(1)}, u32[]{:S(2)}, u32[]{:S(2)}) %collective-permute-start.7) | collective-permute-done | bytes 393248 | tf_op jit(solution)/shard_map/ppermute | solution.py:17
  142.8 0.7 fusion.6
  (35 shorter events, 0.8 us)
Async XLA Ops:
  0.0 6.4 %copy-start.5 = (f32[1,1,1,2,256,256]{5,4,3,2,1,0:T(8,128)S(1)}, f32[1,1,1,2,256,256]{5,4,3,2,1,0:T(8,128)}, u32[]{:S(2)}) copy-start(f32[1,1,1,2,256,256]{5,4,3,2,1,0:T(8,128)} %param.7) | copy-start | bytes 1572868
  0.0 11.3 %collective-permute-start = (f32[2,2,128,128]{3,2,1,0:T(8,128)}, f32[2,2,128,128]{3,2,1,0:T(8,128)S(1)}, u32[]{:S(2)}, u32[]{:S(2)}) collective-permute-start(f32[2,2,128,128]{3,2,1,0:T(8,128)} %param.4), channel_id=1, source_target_pairs={{0,28},{4,0},{8,4},{12,8},{16,12},{20,16},{24,20},{28,24},{1,29},{... | collective-permute-start | bytes 786440 | tf_op jit(solution)/shard_map/ppermute | solution.py:17
  11.3 4.6 %collective-permute-start.1 = (f32[2,2,128,128]{3,2,1,0:T(8,128)S(1)}, f32[2,2,128,128]{3,2,1,0:T(8,128)S(1)}, u32[]{:S(2)}, u32[]{:S(2)}) collective-permute-start(f32[2,2,128,128]{3,2,1,0:T(8,128)S(1)} %collective-permute-done), channel_id=1, source_target_pairs={{0,28},{4,0},{8,4},{12,8},{16,12},{20,16},{24,20},{28,24},{1,29},{... | collective-permute-start | bytes 786440 | tf_op jit(solution)/shard_map/ppermute | solution.py:17
  11.9 1.5 %copy-start.1 = (f32[2,2,128,128]{3,2,1,0:T(8,128)S(1)}, f32[2,2,128,128]{3,2,1,0:T(8,128)}, u32[]{:S(2)}) copy-start(f32[2,2,128,128]{3,2,1,0:T(8,128)} %param.4) | copy-start | bytes 786436
  15.8 20.7 %collective-permute-start.2 = (f32[2,2,384,128]{3,2,1,0:T(8,128)S(1)}, f32[2,2,384,128]{3,2,1,0:T(8,128)S(1)}, u32[]{:S(2)}, u32[]{:S(2)}) collective-permute-start(f32[2,2,384,128]{3,2,1,0:T(8,128)S(1)} %constant_dynamic-update-slice_fusion), channel_id=1, source_target_pairs={{0,3},{1,0},{2,1},{3,2},{4,7},{5,4},{6,5},{7,6},{8,11},{9,8},{10,9... | collective-permute-start | bytes 2359304 | tf_op jit(solution)/shard_map/ppermute | solution.py:17
  21.8 2.1 %copy-start = (f32[2,256,256]{2,1,0:T(8,128)S(1)}, f32[2,256,256]{2,1,0:T(8,128)}, u32[]{:S(2)}) copy-start(f32[2,256,256]{2,1,0:T(8,128)} %param.5) | copy-start | bytes 1572868
  23.9 16.8 %copy-start.4 = (s32[1,1,1,2]{3,2,1,0:T(1,128)S(1)}, s32[1,1,1,2]{3,2,1,0:T(1,128)}, u32[]{:S(2)}) copy-start(s32[1,1,1,2]{3,2,1,0:T(1,128)} %param.6) | copy-start | bytes 28
  36.5 20.2 %collective-permute-start.3 = (f32[2,2,384,128]{3,2,1,0:T(8,128)S(1)}, f32[2,2,384,128]{3,2,1,0:T(8,128)S(1)}, u32[]{:S(2)}, u32[]{:S(2)}) collective-permute-start(f32[2,2,384,128]{3,2,1,0:T(8,128)S(1)} %collective-permute-done.2), channel_id=1, source_target_pairs={{0,3},{1,0},{2,1},{3,2},{4,7},{5,4},{6,5},{7,6},{8,11},{9,8},{10,9... | collective-permute-start | bytes 2359304 | tf_op jit(solution)/shard_map/ppermute | solution.py:17
  45.2 2.5 %copy-start.6 = (f32[1,1,1,2,256,256]{5,4,3,2,1,0:T(8,128)S(1)}, f32[1,1,1,2,256,256]{5,4,3,2,1,0:T(8,128)}, u32[]{:S(2)}) copy-start(f32[1,1,1,2,256,256]{5,4,3,2,1,0:T(8,128)} %param.7) | copy-start | bytes 1572868
  45.2 2.5 %copy-start.8 = (f32[256,256]{1,0:T(8,128)S(1)}, f32[256,256]{1,0:T(8,128)}, u32[]{:S(2)}) copy-start(f32[256,256]{1,0:T(8,128)} %fusion.13) | copy-start | bytes 786436
  47.7 1.4 copy-start.7
  50.5 7.0 %copy-start.3 = (f32[256,256]{1,0:T(8,128)S(1)}, f32[256,256]{1,0:T(8,128)}, u32[]{:S(2)}) copy-start(f32[256,256]{1,0:T(8,128)} %fusion.37) | copy-start | bytes 786436
  87.8 17.3 %collective-permute-start.4 = (f32[2,3,128,384]{3,2,1,0:T(8,128)S(1)}, f32[2,3,128,384]{3,2,1,0:T(8,128)S(1)}, u32[]{:S(2)}, u32[]{:S(2)}) collective-permute-start(f32[2,3,128,384]{3,2,1,0:T(8,128)S(1)} %slice.78), channel_id=1, source_target_pairs={{0,4},{4,8},{8,12},{12,16},{16,20},{20,24},{24,28},{28,0},{1,5},{5... | collective-permute-start | bytes 3538952 | tf_op jit(solution)/shard_map/ppermute | solution.py:17
  105.3 16.6 %collective-permute-start.5 = (f32[2,3,128,384]{3,2,1,0:T(8,128)S(1)}, f32[2,3,128,384]{3,2,1,0:T(8,128)S(1)}, u32[]{:S(2)}, u32[]{:S(2)}) collective-permute-start(f32[2,3,128,384]{3,2,1,0:T(8,128)S(1)} %slice_add_fusion.1), channel_id=1, source_target_pairs={{0,4},{4,8},{8,12},{12,16},{16,20},{20,24},{24,28},{28,0},{1,5},{5... | collective-permute-start | bytes 3538952 | tf_op jit(solution)/shard_map/ppermute | solution.py:17
  122.1 20.7 %copy-start.2 = (f32[2,2,128,128]{3,2,1,0:T(8,128)S(1)}, f32[2,2,128,128]{3,2,1,0:T(8,128)}, u32[]{:S(2)}) copy-start(f32[2,2,128,128]{3,2,1,0:T(8,128)} %param.4) | copy-start | bytes 786436
  122.1 10.2 %collective-permute-start.6 = (f32[2,3,128,128]{3,2,1,0:T(8,128)S(1)}, f32[2,3,128,128]{3,2,1,0:T(8,128)S(1)}, u32[]{:S(2)}, u32[]{:S(2)}) collective-permute-start(f32[2,3,128,128]{3,2,1,0:T(8,128)S(1)} %slice.81), channel_id=1, source_target_pairs={{0,1},{1,2},{2,3},{3,0},{4,5},{5,6},{6,7},{7,4},{8,9},{9,10},{10,1... | collective-permute-start | bytes 1179656 | tf_op jit(solution)/shard_map/ppermute | solution.py:17
  132.4 10.3 %collective-permute-start.7 = (f32[2,3,128,128]{3,2,1,0:T(8,128)S(1)}, f32[2,3,128,128]{3,2,1,0:T(8,128)S(1)}, u32[]{:S(2)}, u32[]{:S(2)}) collective-permute-start(f32[2,3,128,128]{3,2,1,0:T(8,128)S(1)} %slice_add_fusion.3), channel_id=1, source_target_pairs={{0,1},{1,2},{2,3},{3,0},{4,5},{5,6},{6,7},{7,4},{8,9},{9,10},{10,1... | collective-permute-start | bytes 1179656 | tf_op jit(solution)/shard_map/ppermute | solution.py:17
where the time goes:
time: 146 us; the launch traced here: 144 us
  waiting for transfers between devices  73.4 us (50%)
  matrix products  28 us (19%)
  local copies, waits for them, and re-layouts  21.6 us (15%)
  starting transfers between devices  12.8 us (9%)
  between operations  4.18 us (3%)
  other arithmetic  3.56 us (2%)
    ppermute x8, waiting for transfers between devices, passed_along(): return lax.ppermute(value, axis, pairs)  73.4 us
    dynamic_update_slice x1, local copies, waits for them, and re-layouts, local(): lax.dynamic_update_slice(buffer, older + contrib, (zero, zero, top, left))  20.5 us
    ppermute x8, starting transfers between devices, passed_along(): return lax.ppermute(value, axis, pairs)  12.8 us
    dot_general x7, matrix products, complex_dot(): matmul(left_re, right_im) + matmul(left_im, right_re)  8.07 us
    dot_general x7, matrix products, complex_dot(): matmul(left_re, right_re) - matmul(left_im, right_im)  7.11 us
    dot_general x7, matrix products, complex_dot(): matmul(left_im, right_im)  6.86 us
    dot_general x7, matrix products, complex_dot(): matmul(left_im, right_re)  5.95 us
  transfers between devices with their start and end apart: 8, of which 7 were waited for; matrix products, arithmetic and copies ran while one was open for 15% of the time, Pallas kernels for 0%

commit v1 on v0

v1 whole, which is shorter than its diff:
```python
import math

import jax
import jax.numpy as jnp
import numpy as np
from jax import lax
from jax.sharding import PartitionSpec as P

FRESNEL = 40.0
STEP_SIZE = 0.5
REGULAR = 1.0


def moved(value, axis, steps):
    count = lax.axis_size(axis)
    return lax.ppermute(value, axis, [(k, (k + steps) % count) for k in range(count)])


def tables(width):
    index = np.arange(width)
    inverse = np.exp(2j * np.pi / width * (index[:, None] * index[None, :] % width)) / math.sqrt(width)
    freq = np.where(index < width // 2, index, index - width) / width
    phase = FRESNEL * np.pi * freq * freq
    prop = (inverse * np.exp(-1j * phase)[None, :]) @ np.conj(inverse)
    return inverse, prop


def sandwich(mat, wave_re, wave_im):
    re, im = jnp.asarray(mat.real, jnp.float32), jnp.asarray(mat.imag, jnp.float32)
    right = jnp.block([[re, im], [-im, re]])
    left = jnp.block([[re, -im], [im, re]])
    width = re.shape[0]
    dot = lambda a, b: jnp.dot(a, b, precision=lax.Precision.HIGH, preferred_element_type=jnp.float32)
    half = dot(jnp.concatenate([wave_re, wave_im], axis=1), right)
    full = dot(left, jnp.concatenate([half[:, :width], half[:, width:]], axis=0))
    return full[:width], full[width:]


def columns(region, left, width):
    return lax.dynamic_slice_in_dim(region, left, width, axis=2)


def rows(up, own, down, top, width):
    return lax.dynamic_slice_in_dim(jnp.concatenate([up, own, down], axis=1), top, width, axis=1)


def placed(value, at, axis, tile):
    pads = [(0, 0)] * value.ndim
    pads[axis] = (tile, tile)
    return lax.dynamic_slice_in_dim(jnp.pad(value, pads), tile - at, 3 * tile, axis=axis)


def local(object_slices, probe, offsets, residuals):
    layers, _, tile, _ = object_slices.shape
    width = probe.shape[1]
    inverse, prop = tables(width)

    off = [offsets, moved(offsets, "row", 1), moved(offsets, "row", 2)]
    resid = moved(residuals[0, 0, 0], "row", 1)
    tops = [o[0, 0, 0, 0] for o in off]
    lefts = [o[0, 0, 0, 1] for o in off]

    near = [moved(object_slices[s], "col", -1) for s in range(layers)]
    far = [moved(n, "col", -1) for n in near]
    window = []
    for s in range(layers):
        region = jnp.concatenate([object_slices[s], near[s], far[s]], axis=2)
        up = moved(columns(region, lefts[0], width), "row", 1)
        down = moved(columns(region, lefts[2], width), "row", -1)
        window.append(rows(up, columns(region, lefts[1], width), down, tops[1], width))

    back_re, back_im = sandwich(inverse, resid[0], resid[1])

    def shared(terms):
        lifted = placed(terms, tops[1], 1, tile)
        above = moved(lifted[:, :tile], "row", -1)
        below = moved(lifted[:, 2 * tile :], "row", 1)
        strip = (
            placed(above, lefts[0], 2, tile)
            + placed(lifted[:, tile : 2 * tile], lefts[1], 2, tile)
            + placed(below, lefts[2], 2, tile)
        )
        total = strip[:, :, 2 * tile :]
        for band in (1, 0):
            total = moved(total, "col", 1) + strip[:, :, band * tile : (band + 1) * tile]
        return total

    trans_re, trans_im = window[0]
    wave_re, wave_im = sandwich(
        prop, probe[0] * trans_re - probe[1] * trans_im, probe[0] * trans_im + probe[1] * trans_re
    )
    second = shared(
        jnp.stack(
            [
                wave_re * back_re + wave_im * back_im,
                wave_re * back_im - wave_im * back_re,
                wave_re * wave_re + wave_im * wave_im,
            ]
        )
    )
    trans_re, trans_im = window[1]
    pulled_re, pulled_im = sandwich(
        np.conj(prop), trans_re * back_re + trans_im * back_im, trans_re * back_im - trans_im * back_re
    )
    first = shared(
        jnp.stack([probe[0] * pulled_re + probe[1] * pulled_im, probe[0] * pulled_im - probe[1] * pulled_re])
    )

    light = probe[0] * probe[0] + probe[1] * probe[1]
    offs = jnp.stack([o[0, 0, 0] for o in off])
    all_offs = [offs, moved(offs, "col", 1), moved(offs, "col", 2)]
    spread = jnp.pad(light, tile)
    bright = jnp.zeros((tile, tile), jnp.float32)
    for across in range(3):
        for along in range(3):
            at = all_offs[across][along]
            bright += lax.dynamic_slice(
                spread, (tile * (along + 1) - at[0], tile * (across + 1) - at[1]), (tile, tile)
            )
    new0 = object_slices[0] - STEP_SIZE * first / (bright + REGULAR)
    new1 = object_slices[1] - STEP_SIZE * second[:2] / (second[2:] + REGULAR)
    return jnp.stack([new0, new1])


def solution(mesh):
    split = (
        P(None, None, "row", "col"),
        P(),
        P("row", "col", None, None),
        P("row", "col", None, None, None, None),
    )
    return jax.shard_map(local, mesh=mesh, in_specs=split, out_specs=split[0], check_vma=False)
```

time: 146 us -> 96.8 us (0.66); the launches traced: 144 us -> 95.9 us
  waiting for transfers between devices: 73.4 us -> 18.6 us
  between operations: 4.18 us -> 31.8 us
  matrix products: 28 us -> 5.13 us
  starting transfers between devices: 12.8 us -> 25.8 us
  local copies, waits for them, and re-layouts: 21.6 us -> 10.1 us
    ppermute x8 -> x21, waiting for transfers between devices: 73.4 us -> 18.6 us  [moved(): lax.ppermute(value, axis, [(k, (k + steps) % count) for k in range(count)])]
    dot_general x28 -> x12, matrix products: 28 us -> 5.13 us  [sandwich(): jnp.dot(a, b, precision=lax.Precision.HIGH, preferred_element_type=jnp.fl...]
    dynamic_update_slice x1 -> x0, local copies, waits for them, and re-layouts: 20.5 us -> none  [local(): lax.dynamic_update_slice(buffer, older + contrib, (zero, zero, top, left))]
    ppermute x8 -> x21, starting transfers between devices: 12.8 us -> 25.8 us  [moved(): lax.ppermute(value, axis, [(k, (k + steps) % count) for k in range(count)])]
    unnamed x20 -> x28, local copies, waits for them, and re-layouts: 0.08 us -> 4.56 us
    slice x3 -> x9, local copies, waits for them, and re-layouts: 0.75 us -> 4.04 us  [the longest x2 1.93 us: local(): at[0]]
  transfers between devices with their start and end apart: 8 -> 21, of which waited for: 7 -> 7; matrix products, arithmetic and copies ran while one was open for 15% -> 15% of each run, Pallas kernels for 0% -> 0%
where the time goes in v1:
time: 96.8 us; the launch traced here: 95.9 us
  between operations  31.8 us (33%)
  starting transfers between devices  25.8 us (27%)
  waiting for transfers between devices  18.6 us (19%)
  local copies, waits for them, and re-layouts  10.1 us (10%)
  matrix products  5.13 us (5%)
  other arithmetic  4.49 us (5%)
    ppermute x21, starting transfers between devices, moved(): lax.ppermute(value, axis, [(k, (k + steps) % count) for k in range(count)])  25.8 us
    ppermute x21, waiting for transfers between devices, moved(): lax.ppermute(value, axis, [(k, (k + steps) % count) for k in range(count)])  18.6 us
    dot_general x12, matrix products, sandwich(): jnp.dot(a, b, precision=lax.Precision.HIGH, preferred_element_type=jnp.fl...  5.13 us
    unnamed x28, local copies, waits for them, and re-layouts  4.56 us
  transfers between devices with their start and end apart: 21, of which 7 were waited for; matrix products, arithmetic and copies ran while one was open for 15% of the time, Pallas kernels for 0%

profile of v1, /device:TPU:0, one launch (start us, length us, event | category | flops | bytes accessed | tf_op | source)
XLA Modules:
  0.0 95.9 jit_solution(5734070963793798316)
XLA Ops:
  0.0 0.5 collective-permute-start.3
  0.5 2.5 %collective-permute-start.4 = (s32[1,1,1,2]{3,2,1,0:T(1,128)}, s32[1,1,1,2]{3,2,1,0:T(1,128)S(1)}, u32[]{:S(2)}, u32[]{:S(2)}) collective-permute-start(s32[1,1,1,2]{3,2,1,0:T(1,128)} %param.12), channel_id=1, source_target_pairs={{0,8},{4,12},{8,16},{12,20},{16,24},{20,28},{24,0},{28,4},{1,9},{5... | collective-permute-start | bytes 32 | tf_op jit(solution)/shard_map/ppermute | solution.py:16
  3.0 1.0 %slice_bitcast_fusion.16 = (f32[2,128,128]{2,1,0:T(8,128)S(1)}, f32[2,128,128]{2,1,0:T(8,128)S(1)}) fusion(f32[2,2,128,128]{3,2,1,0:T(8,128)} %param.10), kind=kLoop, calls=%fused_computation.124 | loop fusion | bytes 524288 | tf_op jit(solution)/shard_map/squeeze | solution.py:67
  4.0 3.7 %collective-permute-start = (f32[2,128,128]{2,1,0:T(8,128)S(1)}, f32[2,128,128]{2,1,0:T(8,128)S(1)}, u32[]{:S(2)}, u32[]{:S(2)}) collective-permute-start(f32[2,128,128]{2,1,0:T(8,128)S(1)} %get-tuple-element.25), channel_id=1, source_target_pairs={{0,3},{1,0},{2,1},{3,2},{4,7},{5,4},{6,5},{7,6},{8,11},{9,8},{10,9... | collective-permute-start | bytes 393224 | tf_op jit(solution)/shard_map/ppermute | solution.py:16
  7.6 1.0 %collective-permute-start.6 = (f32[2,256,256]{2,1,0:T(8,128)}, f32[2,256,256]{2,1,0:T(8,128)S(1)}, u32[]{:S(2)}, u32[]{:S(2)}) collective-permute-start(f32[2,256,256]{2,1,0:T(8,128)} %bitcast.155), channel_id=1, source_target_pairs={{0,4},{4,8},{8,12},{12,16},{16,20},{20,24},{24,28},{28,0},{1,5},{5... | collective-permute-start | bytes 1572872 | tf_op jit(solution)/shard_map/ppermute | solution.py:16
  8.7 0.4 collective-permute-start.13
  9.1 1.4 %fusion.79 = (s32[1,1,1,1]{3,2,1,0:T(1,128)}, s32[1,1,1,1]{3,2,1,0:T(1,128)}) fusion(s32[1,1,1,2]{3,2,1,0:T(1,128)} %param.12), kind=kLoop, calls=%fused_computation.148 | loop fusion | bytes 16 | tf_op jit(solution)/shard_map/slice | solution.py:118
  15.0 0.6 fusion.81
  15.5 0.6 fusion.80
  16.1 0.5 collective-permute-start.1
  16.6 0.7 pad_add_fusion
  24.5 2.7 %collective-permute-start.12 = (s32[3,2]{1,0:T(4,128)S(1)}, s32[3,2]{1,0:T(4,128)S(1)}, u32[]{:S(2)}, u32[]{:S(2)}) collective-permute-start(s32[3,2]{1,0:T(4,128)S(1)} %pad_add_fusion), channel_id=1, source_target_pairs={{0,2},{1,3},{2,0},{3,1},{4,6},{5,7},{6,4},{7,5},{8,10},{9,11},{10,... | collective-permute-start | bytes 80 | tf_op jit(solution)/shard_map/ppermute | solution.py:16
  31.6 0.7 fusion.78
  32.2 3.8 %collective-permute-start.14 = (f32[2,128,128]{2,1,0:T(8,128)S(1)}, f32[2,128,128]{2,1,0:T(8,128)S(1)}, u32[]{:S(2)}, u32[]{:S(2)}) collective-permute-start(f32[2,128,128]{2,1,0:T(8,128)S(1)} %collective-permute-done.13), channel_id=1, source_target_pairs={{0,3},{1,0},{2,1},{3,2},{4,7},{5,4},{6,5},{7,6},{8,11},{9,8},{10,9... | collective-permute-start | bytes 393224 | tf_op jit(solution)/shard_map/ppermute | solution.py:16
  36.4 2.6 %collective-permute-start.5 = (f32[2,128,256]{2,1,0:T(8,128)S(1)}, f32[2,128,256]{2,1,0:T(8,128)S(1)}, u32[]{:S(2)}, u32[]{:S(2)}) collective-permute-start(f32[2,128,256]{2,1,0:T(8,128)S(1)} %get-tuple-element.17), channel_id=1, source_target_pairs={{0,28},{4,0},{8,4},{12,8},{16,12},{20,16},{24,20},{28,24},{1,29},{... | collective-permute-start | bytes 786440 | tf_op jit(solution)/shard_map/ppermute | solution.py:16
  39.5 2.6 %collective-permute-start.16 = (f32[2,128,256]{2,1,0:T(8,128)S(1)}, f32[2,128,256]{2,1,0:T(8,128)S(1)}, u32[]{:S(2)}, u32[]{:S(2)}) collective-permute-start(f32[2,128,256]{2,1,0:T(8,128)S(1)} %get-tuple-element.20), channel_id=1, source_target_pairs={{0,28},{4,0},{8,4},{12,8},{16,12},{20,16},{24,20},{28,24},{1,29},{... | collective-permute-start | bytes 786440 | tf_op jit(solution)/shard_map/ppermute | solution.py:16
  42.1 0.6 fusion.32
  42.8 0.6 fusion
  43.4 0.4 copy-done.10
  43.8 0.4 fusion.30
  44.2 0.4 convolution_add_fusion.4
  44.6 0.5 collective-permute-done.2
  45.1 0.7 collective-permute-done.5
  46.0 0.4 fusion.46
  46.4 0.4 copy-done.13
  46.8 0.4 convolution_add_fusion.3
  47.2 0.6 copy-done.9
  48.2 0.7 copy-done.4
  48.9 0.4 convolution_add_fusion.2
  49.3 0.6 copy-done
  50.0 0.7 collective-permute-done.15
  51.0 0.4 fusion.39
  51.4 0.4 copy-done.12
  51.8 0.4 convolution_add_fusion.1
  52.2 0.6 copy-done.8
  53.2 0.7 copy-done.2
  53.9 0.4 convolution_add_fusion
  54.8 2.5 %collective-permute-start.17 = (f32[3,128,256]{2,1,0:T(8,128)S(1)}, f32[3,128,256]{2,1,0:T(8,128)S(1)}, u32[]{:S(2)}, u32[]{:S(2)}) collective-permute-start(f32[3,128,256]{2,1,0:T(8,128)S(1)} %get-tuple-element.7), channel_id=1, source_target_pairs={{0,28},{4,0},{8,4},{12,8},{16,12},{20,16},{24,20},{28,24},{1,29},{... | collective-permute-start | bytes 1179656 | tf_op jit(solution)/shard_map/ppermute | solution.py:16
  57.5 2.7 %collective-permute-start.7 = (f32[2,128,256]{2,1,0:T(8,128)S(1)}, f32[2,128,256]{2,1,0:T(8,128)S(1)}, u32[]{:S(2)}, u32[]{:S(2)}) collective-permute-start(f32[2,128,256]{2,1,0:T(8,128)S(1)} %get-tuple-element.14), channel_id=1, source_target_pairs={{0,28},{4,0},{8,4},{12,8},{16,12},{20,16},{24,20},{28,24},{1,29},{... | collective-permute-start | bytes 786440 | tf_op jit(solution)/shard_map/ppermute | solution.py:16
  60.2 0.7 fusion.77
  76.1 0.5 fusion.16
  76.8 0.8 fusion.74
  77.7 0.4 fusion.22
  78.1 7.8 %collective-permute-done.19 = f32[3,128,128]{2,1,0:T(8,128)S(1)} collective-permute-done((f32[3,128,128]{2,1,0:T(8,128)S(1)}, f32[3,128,128]{2,1,0:T(8,128)S(1)}, u32[]{:S(2)}, u32[]{:S(2)}) %collective-permute-start.19) | collective-permute-done | bytes 196640 | tf_op jit(solution)/shard_map/ppermute | solution.py:16
  86.1 1.3 %collective-permute-done.9 = f32[2,128,128]{2,1,0:T(8,128)S(1)} collective-permute-done((f32[2,128,128]{2,1,0:T(8,128)S(1)}, f32[2,128,128]{2,1,0:T(8,128)S(1)}, u32[]{:S(2)}, u32[]{:S(2)}) %collective-permute-start.9) | collective-permute-done | bytes 131104 | tf_op jit(solution)/shard_map/ppermute | solution.py:16
  87.5 6.2 %collective-permute-done.20 = f32[3,128,128]{2,1,0:T(8,128)S(1)} collective-permute-done((f32[3,128,128]{2,1,0:T(8,128)S(1)}, f32[3,128,128]{2,1,0:T(8,128)S(1)}, u32[]{:S(2)}, u32[]{:S(2)}) %collective-permute-start.20) | collective-permute-done | bytes 196640 | tf_op jit(solution)/shard_map/ppermute | solution.py:16
  93.7 1.4 %collective-permute-done.10 = f32[2,128,128]{2,1,0:T(8,128)S(1)} collective-permute-done((f32[2,128,128]{2,1,0:T(8,128)S(1)}, f32[2,128,128]{2,1,0:T(8,128)S(1)}, u32[]{:S(2)}, u32[]{:S(2)}) %collective-permute-start.10) | collective-permute-done | bytes 131104 | tf_op jit(solution)/shard_map/ppermute | solution.py:16
  95.2 0.7 pad_maximum_fusion.2
  (64 shorter events, 3.3 us)
Async XLA Ops:
  0.0 14.9 %collective-permute-start.3 = (s32[1,1,1,2]{3,2,1,0:T(1,128)}, s32[1,1,1,2]{3,2,1,0:T(1,128)S(1)}, u32[]{:S(2)}, u32[]{:S(2)}) collective-permute-start(s32[1,1,1,2]{3,2,1,0:T(1,128)} %param.12), channel_id=1, source_target_pairs={{0,4},{4,8},{8,12},{12,16},{16,20},{20,24},{24,28},{28,0},{1,5},{5... | collective-permute-start | bytes 32 | tf_op jit(solution)/shard_map/ppermute | solution.py:16
  0.5 15.0 %collective-permute-start.4 = (s32[1,1,1,2]{3,2,1,0:T(1,128)}, s32[1,1,1,2]{3,2,1,0:T(1,128)S(1)}, u32[]{:S(2)}, u32[]{:S(2)}) collective-permute-start(s32[1,1,1,2]{3,2,1,0:T(1,128)} %param.12), channel_id=1, source_target_pairs={{0,8},{4,12},{8,16},{12,20},{16,24},{20,28},{24,0},{28,4},{1,9},{5... | collective-permute-start | bytes 32 | tf_op jit(solution)/shard_map/ppermute | solution.py:16
  4.0 12.1 %collective-permute-start = (f32[2,128,128]{2,1,0:T(8,128)S(1)}, f32[2,128,128]{2,1,0:T(8,128)S(1)}, u32[]{:S(2)}, u32[]{:S(2)}) collective-permute-start(f32[2,128,128]{2,1,0:T(8,128)S(1)} %get-tuple-element.25), channel_id=1, source_target_pairs={{0,3},{1,0},{2,1},{3,2},{4,7},{5,4},{6,5},{7,6},{8,11},{9,8},{10,9... | collective-permute-start | bytes 393224 | tf_op jit(solution)/shard_map/ppermute | solution.py:16
  7.6 31.9 %collective-permute-start.6 = (f32[2,256,256]{2,1,0:T(8,128)}, f32[2,256,256]{2,1,0:T(8,128)S(1)}, u32[]{:S(2)}, u32[]{:S(2)}) collective-permute-start(f32[2,256,256]{2,1,0:T(8,128)} %bitcast.155), channel_id=1, source_target_pairs={{0,4},{4,8},{8,12},{12,16},{16,20},{20,24},{24,28},{28,0},{1,5},{5... | collective-permute-start | bytes 1572872 | tf_op jit(solution)/shard_map/ppermute | solution.py:16
  8.7 23.6 %collective-permute-start.13 = (f32[2,128,128]{2,1,0:T(8,128)S(1)}, f32[2,128,128]{2,1,0:T(8,128)S(1)}, u32[]{:S(2)}, u32[]{:S(2)}) collective-permute-start(f32[2,128,128]{2,1,0:T(8,128)S(1)} %get-tuple-element.26), channel_id=1, source_target_pairs={{0,3},{1,0},{2,1},{3,2},{4,7},{5,4},{6,5},{7,6},{8,11},{9,8},{10,9... | collective-permute-start | bytes 393224 | tf_op jit(solution)/shard_map/ppermute | solution.py:16
  16.1 19.9 %collective-permute-start.1 = (f32[2,128,128]{2,1,0:T(8,128)S(1)}, f32[2,128,128]{2,1,0:T(8,128)S(1)}, u32[]{:S(2)}, u32[]{:S(2)}) collective-permute-start(f32[2,128,128]{2,1,0:T(8,128)S(1)} %collective-permute-done), channel_id=1, source_target_pairs={{0,3},{1,0},{2,1},{3,2},{4,7},{5,4},{6,5},{7,6},{8,11},{9,8},{10,9... | collective-permute-start | bytes 393224 | tf_op jit(solution)/shard_map/ppermute | solution.py:16
  24.5 7.0 %collective-permute-start.12 = (s32[3,2]{1,0:T(4,128)S(1)}, s32[3,2]{1,0:T(4,128)S(1)}, u32[]{:S(2)}, u32[]{:S(2)}) collective-permute-start(s32[3,2]{1,0:T(4,128)S(1)} %pad_add_fusion), channel_id=1, source_target_pairs={{0,2},{1,3},{2,0},{3,1},{4,6},{5,7},{6,4},{7,5},{8,10},{9,11},{10,... | collective-permute-start | bytes 80 | tf_op jit(solution)/shard_map/ppermute | solution.py:16
  27.2 33.1 %collective-permute-start.11 = (s32[3,2]{1,0:T(4,128)S(1)}, s32[3,2]{1,0:T(4,128)S(1)}, u32[]{:S(2)}, u32[]{:S(2)}) collective-permute-start(s32[3,2]{1,0:T(4,128)S(1)} %pad_add_fusion), channel_id=1, source_target_pairs={{0,1},{1,2},{2,3},{3,0},{4,5},{5,6},{6,7},{7,4},{8,9},{9,10},{10,1... | collective-permute-start | bytes 80 | tf_op jit(solution)/shard_map/ppermute | solution.py:16
  32.2 6.8 %collective-permute-start.14 = (f32[2,128,128]{2,1,0:T(8,128)S(1)}, f32[2,128,128]{2,1,0:T(8,128)S(1)}, u32[]{:S(2)}, u32[]{:S(2)}) collective-permute-start(f32[2,128,128]{2,1,0:T(8,128)S(1)} %collective-permute-done.13), channel_id=1, source_target_pairs={{0,3},{1,0},{2,1},{3,2},{4,7},{5,4},{6,5},{7,6},{8,11},{9,8},{10,9... | collective-permute-start | bytes 393224 | tf_op jit(solution)/shard_map/ppermute | solution.py:16
  36.4 8.7 %collective-permute-start.2 = (f32[2,128,256]{2,1,0:T(8,128)S(1)}, f32[2,128,256]{2,1,0:T(8,128)S(1)}, u32[]{:S(2)}, u32[]{:S(2)}) collective-permute-start(f32[2,128,256]{2,1,0:T(8,128)S(1)} %get-tuple-element.19), channel_id=1, source_target_pairs={{0,4},{4,8},{8,12},{12,16},{16,20},{20,24},{24,28},{28,0},{1,5},{5... | collective-permute-start | bytes 786440 | tf_op jit(solution)/shard_map/ppermute | solution.py:16
  36.4 5.7 %copy-start.11 = (f32[256,512]{1,0:T(8,128)S(1)}, f32[256,512]{1,0:T(8,128)}, u32[]{:S(2)}) copy-start(f32[256,512]{1,0:T(8,128)} %constant.137) | copy-start | bytes 1572868
  36.4 9.3 %collective-permute-start.5 = (f32[2,128,256]{2,1,0:T(8,128)S(1)}, f32[2,128,256]{2,1,0:T(8,128)S(1)}, u32[]{:S(2)}, u32[]{:S(2)}) collective-permute-start(f32[2,128,256]{2,1,0:T(8,128)S(1)} %get-tuple-element.17), channel_id=1, source_target_pairs={{0,28},{4,0},{8,4},{12,8},{16,12},{20,16},{24,20},{28,24},{1,29},{... | collective-permute-start | bytes 786440 | tf_op jit(solution)/shard_map/ppermute | solution.py:16
  39.1 3.6 %copy-start.7 = (f32[256,512]{1,0:T(8,128)S(1)}, f32[256,512]{1,0:T(8,128)}, u32[]{:S(2)}) copy-start(f32[256,512]{1,0:T(8,128)} %constant.136) | copy-start | bytes 1572868
  39.4 11.3 %collective-permute-start.15 = (f32[2,128,256]{2,1,0:T(8,128)S(1)}, f32[2,128,256]{2,1,0:T(8,128)S(1)}, u32[]{:S(2)}, u32[]{:S(2)}) collective-permute-start(f32[2,128,256]{2,1,0:T(8,128)S(1)} %get-tuple-element.22), channel_id=1, source_target_pairs={{0,4},{4,8},{8,12},{12,16},{16,20},{20,24},{24,28},{28,0},{1,5},{5... | collective-permute-start | bytes 786440 | tf_op jit(solution)/shard_map/ppermute | solution.py:16
  39.5 11.2 %collective-permute-start.16 = (f32[2,128,256]{2,1,0:T(8,128)S(1)}, f32[2,128,256]{2,1,0:T(8,128)S(1)}, u32[]{:S(2)}, u32[]{:S(2)}) collective-permute-start(f32[2,128,256]{2,1,0:T(8,128)S(1)} %get-tuple-element.20), channel_id=1, source_target_pairs={{0,28},{4,0},{8,4},{12,8},{16,12},{20,16},{24,20},{28,24},{1,29},{... | collective-permute-start | bytes 786440 | tf_op jit(solution)/shard_map/ppermute | solution.py:16
  42.7 1.0 %copy-start.10 = (f32[512,256]{1,0:T(8,128)S(1)}, f32[512,256]{1,0:T(8,128)}, u32[]{:S(2)}) copy-start(f32[512,256]{1,0:T(8,128)} %constant.135) | copy-start | bytes 1572868
  42.7 1.5 %copy-start.6 = (f32[512,256]{1,0:T(8,128)S(1)}, f32[512,256]{1,0:T(8,128)}, u32[]{:S(2)}) copy-start(f32[512,256]{1,0:T(8,128)} %constant.138) | copy-start | bytes 1572868
  44.2 1.8 %copy-start.5 = (f32[256,512]{1,0:T(8,128)S(1)}, f32[256,512]{1,0:T(8,128)}, u32[]{:S(2)}) copy-start(f32[256,512]{1,0:T(8,128)} %constant.139) | copy-start | bytes 1572868
  45.8 1.0 %copy-start.13 = (f32[256,512]{1,0:T(8,128)S(1)}, f32[256,512]{1,0:T(8,128)}, u32[]{:S(2)}) copy-start(f32[256,512]{1,0:T(8,128)} %constant.140) | copy-start | bytes 1572868
  46.8 1.0 %copy-start.9 = (f32[512,256]{1,0:T(8,128)S(1)}, f32[512,256]{1,0:T(8,128)}, u32[]{:S(2)}) copy-start(f32[512,256]{1,0:T(8,128)} %constant.134) | copy-start | bytes 1572868
  47.8 1.0 %copy-start.4 = (f32[512,256]{1,0:T(8,128)S(1)}, f32[512,256]{1,0:T(8,128)}, u32[]{:S(2)}) copy-start(f32[512,256]{1,0:T(8,128)} %constant.141) | copy-start | bytes 1572868
  48.9 1.0 %copy-start = (f32[2,256,256]{2,1,0:T(8,128)S(1)}, f32[2,256,256]{2,1,0:T(8,128)}, u32[]{:S(2)}) copy-start(f32[2,256,256]{2,1,0:T(8,128)} %param.11) | copy-start | bytes 1572868
  49.9 1.0 %copy-start.3 = (f32[256,512]{1,0:T(8,128)S(1)}, f32[256,512]{1,0:T(8,128)}, u32[]{:S(2)}) copy-start(f32[256,512]{1,0:T(8,128)} %constant.143) | copy-start | bytes 1572868
  50.7 1.1 %copy-start.12 = (f32[256,512]{1,0:T(8,128)S(1)}, f32[256,512]{1,0:T(8,128)}, u32[]{:S(2)}) copy-start(f32[256,512]{1,0:T(8,128)} %constant.144) | copy-start | bytes 1572868
  51.8 1.0 %copy-start.8 = (f32[512,256]{1,0:T(8,128)S(1)}, f32[512,256]{1,0:T(8,128)}, u32[]{:S(2)}) copy-start(f32[512,256]{1,0:T(8,128)} %constant.142) | copy-start | bytes 1572868
  52.8 1.0 %copy-start.2 = (f32[512,256]{1,0:T(8,128)S(1)}, f32[512,256]{1,0:T(8,128)}, u32[]{:S(2)}) copy-start(f32[512,256]{1,0:T(8,128)} %constant.145) | copy-start | bytes 1572868
  54.8 21.3 %collective-permute-start.17 = (f32[3,128,256]{2,1,0:T(8,128)S(1)}, f32[3,128,256]{2,1,0:T(8,128)S(1)}, u32[]{:S(2)}, u32[]{:S(2)}) collective-permute-start(f32[3,128,256]{2,1,0:T(8,128)S(1)} %get-tuple-element.7), channel_id=1, source_target_pairs={{0,28},{4,0},{8,4},{12,8},{16,12},{20,16},{24,20},{28,24},{1,29},{... | collective-permute-start | bytes 1179656 | tf_op jit(solution)/shard_map/ppermute | solution.py:16
  57.3 18.9 %collective-permute-start.18 = (f32[3,128,256]{2,1,0:T(8,128)S(1)}, f32[3,128,256]{2,1,0:T(8,128)S(1)}, u32[]{:S(2)}, u32[]{:S(2)}) collective-permute-start(f32[3,128,256]{2,1,0:T(8,128)S(1)} %get-tuple-element.5), channel_id=1, source_target_pairs={{0,4},{4,8},{8,12},{12,16},{16,20},{20,24},{24,28},{28,0},{1,5},{5... | collective-permute-start | bytes 1179656 | tf_op jit(solution)/shard_map/ppermute | solution.py:16
  57.5 20.1 %collective-permute-start.7 = (f32[2,128,256]{2,1,0:T(8,128)S(1)}, f32[2,128,256]{2,1,0:T(8,128)S(1)}, u32[]{:S(2)}, u32[]{:S(2)}) collective-permute-start(f32[2,128,256]{2,1,0:T(8,128)S(1)} %get-tuple-element.14), channel_id=1, source_target_pairs={{0,28},{4,0},{8,4},{12,8},{16,12},{20,16},{24,20},{28,24},{1,29},{... | collective-permute-start | bytes 786440 | tf_op jit(solution)/shard_map/ppermute | solution.py:16
  60.2 17.4 %collective-permute-start.8 = (f32[2,128,256]{2,1,0:T(8,128)S(1)}, f32[2,128,256]{2,1,0:T(8,128)S(1)}, u32[]{:S(2)}, u32[]{:S(2)}) collective-permute-start(f32[2,128,256]{2,1,0:T(8,128)S(1)} %get-tuple-element.12), channel_id=1, source_target_pairs={{0,4},{4,8},{8,12},{12,16},{16,20},{20,24},{24,28},{28,0},{1,5},{5... | collective-permute-start | bytes 786440 | tf_op jit(solution)/shard_map/ppermute | solution.py:16
  76.7 9.3 %collective-permute-start.19 = (f32[3,128,128]{2,1,0:T(8,128)S(1)}, f32[3,128,128]{2,1,0:T(8,128)S(1)}, u32[]{:S(2)}, u32[]{:S(2)}) collective-permute-start(f32[3,128,128]{2,1,0:T(8,128)S(1)} %slice.289), channel_id=1, source_target_pairs={{0,1},{1,2},{2,3},{3,0},{4,5},{5,6},{6,7},{7,4},{8,9},{9,10},{10,1... | collective-permute-start | bytes 589832 | tf_op jit(solution)/shard_map/ppermute | solution.py:16
  78.1 17.1 %copy-start.1 = (f32[2,2,128,128]{3,2,1,0:T(8,128)S(1)}, f32[2,2,128,128]{3,2,1,0:T(8,128)}, u32[]{:S(2)}) copy-start(f32[2,2,128,128]{3,2,1,0:T(8,128)} %param.10) | copy-start | bytes 786436
  78.1 9.3 %collective-permute-start.9 = (f32[2,128,128]{2,1,0:T(8,128)S(1)}, f32[2,128,128]{2,1,0:T(8,128)S(1)}, u32[]{:S(2)}, u32[]{:S(2)}) collective-permute-start(f32[2,128,128]{2,1,0:T(8,128)S(1)} %slice.279), channel_id=1, source_target_pairs={{0,1},{1,2},{2,3},{3,0},{4,5},{5,6},{6,7},{7,4},{8,9},{9,10},{10,1... | collective-permute-start | bytes 393224 | tf_op jit(solution)/shard_map/ppermute | solution.py:16
  86.0 7.7 %collective-permute-start.20 = (f32[3,128,128]{2,1,0:T(8,128)S(1)}, f32[3,128,128]{2,1,0:T(8,128)S(1)}, u32[]{:S(2)}, u32[]{:S(2)}) collective-permute-start(f32[3,128,128]{2,1,0:T(8,128)S(1)} %slice_add_fusion.1), channel_id=1, source_target_pairs={{0,1},{1,2},{2,3},{3,0},{4,5},{5,6},{6,7},{7,4},{8,9},{9,10},{10,1... | collective-permute-start | bytes 589832 | tf_op jit(solution)/shard_map/ppermute | solution.py:16
  87.4 7.7 %collective-permute-start.10 = (f32[2,128,128]{2,1,0:T(8,128)S(1)}, f32[2,128,128]{2,1,0:T(8,128)S(1)}, u32[]{:S(2)}, u32[]{:S(2)}) collective-permute-start(f32[2,128,128]{2,1,0:T(8,128)S(1)} %slice_add_fusion.3), channel_id=1, source_target_pairs={{0,1},{1,2},{2,3},{3,0},{4,5},{5,6},{6,7},{7,4},{8,9},{9,10},{10,1... | collective-permute-start | bytes 393224 | tf_op jit(solution)/shard_map/ppermute | solution.py:16

commit v2 on v1

v2 whole, which is shorter than its diff:
```python
import functools
import math

import jax
import jax.numpy as jnp
import numpy as np
from jax import lax
from jax.experimental import pallas as pl
from jax.experimental.pallas import tpu as pltpu
from jax.sharding import PartitionSpec as P

FRESNEL = 40.0
STEP_SIZE = 0.5
REGULAR = 1.0
VMEM_BYTES = 16 * 2**20
VMEM = pl.BlockSpec(memory_space=pltpu.VMEM)
SMEM = pl.BlockSpec(memory_space=pltpu.SMEM)


def moved(value, axis, steps):
    count = lax.axis_size(axis)
    return lax.ppermute(value, axis, [(k, (k + steps) % count) for k in range(count)])


def call(body, name, out_shapes, ins, scratch=()):
    return pl.pallas_call(
        body,
        name=name,
        out_shape=[jax.ShapeDtypeStruct(s, d) for s, d in out_shapes],
        in_specs=[SMEM if v.dtype == jnp.int32 else VMEM for v in ins],
        out_specs=[VMEM] * len(out_shapes),
        scratch_shapes=list(scratch),
        compiler_params=pltpu.CompilerParams(vmem_limit_bytes=VMEM_BYTES),
    )(*ins)


def halves(value):
    high = value.astype(jnp.bfloat16)
    return high, (value - high.astype(jnp.float32)).astype(jnp.bfloat16)


def tables(width):
    index = np.arange(width)
    inverse = np.exp(2j * np.pi / width * (index[:, None] * index[None, :] % width)) / math.sqrt(width)
    freq = np.where(index < width // 2, index, index - width) / width
    phase = FRESNEL * np.pi * freq * freq
    prop = (inverse * np.exp(-1j * phase)[None, :]) @ np.conj(inverse)

    def packed(mat):
        parts = []
        for part in (mat.real, mat.imag):
            part = part.astype(np.float32)
            high = part.astype(jnp.bfloat16)
            parts.append(np.stack([high, (part - high.astype(np.float32)).astype(jnp.bfloat16)]))
        return jnp.asarray(np.stack(parts))

    return packed(inverse), packed(prop)


def dot3(left, right):
    dot = functools.partial(jnp.dot, preferred_element_type=jnp.float32)
    return dot(left[0], right[0]) + dot(left[1], right[0]) + dot(left[0], right[1])


def sandwich(mat_ref, sign, wave_re, wave_im):
    mat_re = (mat_ref[0, 0], mat_ref[0, 1])
    mat_im = (mat_ref[1, 0], mat_ref[1, 1])
    wave_re, wave_im = halves(wave_re), halves(wave_im)
    half_re = dot3(wave_re, mat_re) - sign * dot3(wave_im, mat_im)
    half_im = dot3(wave_im, mat_re) + sign * dot3(wave_re, mat_im)
    half_re, half_im = halves(half_re), halves(half_im)
    return (
        dot3(mat_re, half_re) - sign * dot3(mat_im, half_im),
        dot3(mat_re, half_im) + sign * dot3(mat_im, half_re),
    )


def lanes(shape):
    return lax.broadcasted_iota(jnp.int32, shape, len(shape) - 1)


def turned(value, by):
    return pltpu.roll(value, by, value.ndim - 1)


def back_body(resid_ref, mat_ref, back_ref):
    back_ref[0], back_ref[1] = sandwich(mat_ref, 1.0, resid_ref[0], resid_ref[1])


def spread_body(off0, off1, off2, own_ref, near_ref, far_ref, up_ref, mid_ref, down_ref):
    tile = own_ref.shape[-1]
    for off, out_ref in ((off0, up_ref), (off1, mid_ref), (off2, down_ref)):
        left = off[0, 1]
        by = lax.select(left == 0, 0, tile - left)
        keep = lanes((tile, tile)) < tile - left
        for part in range(own_ref.shape[0]):
            first, second, third = (turned(ref[part], by) for ref in (own_ref, near_ref, far_ref))
            out_ref[part, :, :tile] = jnp.where(keep, first, second)
            out_ref[part, :, tile:] = jnp.where(keep, second, third)


def rows_at(ref, start, count):
    rest = lax.rem(start, 8)
    value = ref[pl.ds(pl.multiple_of(start - rest, 8), count + 8)]
    value = value.reshape(count // 8 + 1, 8, value.shape[-1])
    value = pltpu.roll(value, lax.rem(8 - rest, 8), 1)
    keep = lax.broadcasted_iota(jnp.int32, value[1:].shape, 1) < 8 - rest
    return jnp.where(keep, value[:-1], value[1:]).reshape(count, value.shape[-1])


def rows_to(ref, start, value):
    count, width = value.shape
    rest = lax.rem(start, 8)
    value = pltpu.roll(value.reshape(count // 8, 8, width), rest, 1)
    none = jnp.zeros((1, 8, width), value.dtype)
    now, before = jnp.concatenate([value, none], axis=0), jnp.concatenate([none, value], axis=0)
    keep = lax.broadcasted_iota(jnp.int32, now.shape, 1) >= rest
    ref[pl.ds(pl.multiple_of(start - rest, 8), count + 8)] = jnp.where(keep, now, before).reshape(count + 8, width)


def windowed(tall_ref, top, up_ref, mid_ref, down_ref):
    tile, width = up_ref.shape[1:]
    for band, ref in enumerate((up_ref, mid_ref, down_ref)):
        tall_ref[:2, band * tile : (band + 1) * tile] = ref[...]
    return rows_at(tall_ref.at[0], top, width), rows_at(tall_ref.at[1], top, width)


def handed_out(tall_ref, top, terms, outs):
    tile, width = outs[0].shape[1:]
    zeros = jnp.zeros((tile, width), jnp.float32)
    for part, term in enumerate(terms):
        tall_ref[part, :tile] = zeros
        tall_ref[part, 2 * tile :] = zeros
        rows_to(tall_ref.at[part], top, term)
        for band, out_ref in enumerate(outs):
            out_ref[part] = tall_ref[part, band * tile : (band + 1) * tile]


def wave_body(off1, up_ref, mid_ref, down_ref, probe_ref, back_ref, mat_ref, out0, out1, out2, tall_ref):
    top = off1[0, 0]
    trans_re, trans_im = windowed(tall_ref, top, up_ref, mid_ref, down_ref)
    probe_re, probe_im = probe_ref[0], probe_ref[1]
    wave_re, wave_im = sandwich(
        mat_ref, 1.0, probe_re * trans_re - probe_im * trans_im, probe_re * trans_im + probe_im * trans_re
    )
    back_re, back_im = back_ref[0], back_ref[1]
    terms = (
        wave_re * back_re + wave_im * back_im,
        wave_re * back_im - wave_im * back_re,
        wave_re * wave_re + wave_im * wave_im,
    )
    handed_out(tall_ref, top, terms, (out0, out1, out2))


def pull_body(off1, up_ref, mid_ref, down_ref, probe_ref, back_ref, mat_ref, out0, out1, out2, tall_ref):
    top = off1[0, 0]
    trans_re, trans_im = windowed(tall_ref, top, up_ref, mid_ref, down_ref)
    back_re, back_im = back_ref[0], back_ref[1]
    pulled_re, pulled_im = sandwich(
        mat_ref, -1.0, trans_re * back_re + trans_im * back_im, trans_re * back_im - trans_im * back_re
    )
    probe_re, probe_im = probe_ref[0], probe_ref[1]
    terms = (probe_re * pulled_re + probe_im * pulled_im, probe_re * pulled_im - probe_im * pulled_re)
    handed_out(tall_ref, top, terms, (out0, out1, out2))


def merge_body(off0, off1, off2, above_ref, mid_ref, below_ref, out0, out1, out2):
    tile = out0.shape[-1]
    for part in range(out0.shape[0]):
        totals = [jnp.zeros((tile, tile), jnp.float32) for _ in range(3)]
        for off, ref in ((off0, above_ref), (off1, mid_ref), (off2, below_ref)):
            left = off[0, 1]
            first, second = turned(ref[part, :, :tile], left), turned(ref[part, :, tile:], left)
            inside = lanes((tile, tile)) >= left
            totals[0] += jnp.where(inside, first, 0.0)
            totals[1] += jnp.where(inside, second, first)
            totals[2] += jnp.where(inside, 0.0, second)
        out0[part], out1[part], out2[part] = totals


def bright_body(offs0, offs1, offs2, probe_ref, out_ref, tall_ref):
    tile = out_ref.shape[-1]
    width = probe_ref.shape[-1]
    tall_ref[:tile] = jnp.zeros((tile, width), jnp.float32)
    tall_ref[tile + width :] = jnp.zeros((tile + 8, width), jnp.float32)
    tall_ref[tile : tile + width] = probe_ref[0] * probe_ref[0] + probe_ref[1] * probe_ref[1]
    total = jnp.zeros((tile, tile), jnp.float32)
    for across, offs in enumerate((offs0, offs1, offs2)):
        for along in range(3):
            top, left = offs[along, 0], offs[along, 1]
            strip = rows_at(tall_ref, tile * (along + 1) - top, tile)
            inside = lanes((tile, tile)) >= left
            first, second = turned(strip[:, :tile], left), turned(strip[:, tile:], left)
            if across == 0:
                total += jnp.where(inside, first, 0.0)
            elif across == 1:
                total += jnp.where(inside, second, first)
            else:
                total += jnp.where(inside, 0.0, second)
    out_ref[...] = total


def joined_body(off0, off1, off2, out_ref):
    for along, off in enumerate((off0, off1, off2)):
        out_ref[along, 0] = off[0, 0]
        out_ref[along, 1] = off[0, 1]


def local(object_slices, probe, offsets, residuals):
    layers, _, tile, _ = object_slices.shape
    width = probe.shape[1]
    inverse, prop = tables(width)
    f32 = jnp.float32

    off = offsets.reshape(1, 2)
    off = [off, moved(off, "row", 1), moved(off, "row", 2)]
    near = [moved(object_slices[s], "col", -1) for s in range(layers)]
    resid = moved(residuals.reshape(2, width, width), "row", 1)
    far = [moved(n, "col", -1) for n in near]

    (back,) = call(back_body, "back", [((2, width, width), f32)], [resid, inverse])

    def window(s):
        strip = ((2, tile, width), f32)
        up, mid, down = call(spread_body, "spread", [strip] * 3, [*off, object_slices[s], near[s], far[s]])
        return moved(up, "row", 1), mid, moved(down, "row", -1)

    def terms(body, name, parts, strips):
        tall = pltpu.VMEM((3, 3 * tile, width), f32)
        strip = ((parts, tile, width), f32)
        return call(body, name, [strip] * 3, [off[1], *strips, probe, back, prop], [tall])

    def shared(lifted):
        above, below = moved(lifted[0], "row", -1), moved(lifted[2], "row", 1)
        band = (lifted[1].shape[0], tile, tile)
        first, second, third = call(merge_body, "merge", [(band, f32)] * 3, [*off, above, lifted[1], below])
        return first + moved(second + moved(third, "col", 1), "col", 1)

    strips = [window(s) for s in range(layers)]
    second = shared(terms(wave_body, "wave", 3, strips[0]))
    first = shared(terms(pull_body, "pull", 2, strips[1]))

    offs = pl.pallas_call(
        joined_body,
        name="joined",
        out_shape=jax.ShapeDtypeStruct((3, 2), jnp.int32),
        in_specs=[SMEM] * 3,
        out_specs=SMEM,
        compiler_params=pltpu.CompilerParams(vmem_limit_bytes=VMEM_BYTES),
    )(*off)
    tall = pltpu.VMEM((2 * tile + width + 8, width), f32)
    (bright,) = call(
        bright_body, "bright", [((tile, tile), f32)], [offs, moved(offs, "col", 1), moved(offs, "col", 2), probe], [tall]
    )

    new0 = object_slices[0] - STEP_SIZE * first / (bright + REGULAR)
    new1 = object_slices[1] - STEP_SIZE * second[:2] / (second[2:] + REGULAR)
    return jnp.stack([new0, new1])


def solution(mesh):
    split = (
        P(None, None, "row", "col"),
        P(),
        P("row", "col", None, None),
        P("row", "col", None, None, None, None),
    )
    return jax.shard_map(local, mesh=mesh, in_specs=split, out_specs=split[0], check_vma=False)
```

time: 96.8 us -> 80.9 us (0.84)
  between operations: 31.8 us -> 0.2 us
  waiting for transfers between devices: 18.6 us -> 37.7 us
  Pallas kernels: 0 us -> 10.7 us
  local copies, waits for them, and re-layouts: 10.1 us -> 1.06 us
  matrix products: 5.13 us -> 0 us
  starting transfers between devices: 25.8 us -> 30.2 us
  other arithmetic: 4.49 us -> 0.84 us
    ppermute x21, waiting for transfers between devices: 18.6 us -> 37.7 us  [moved(): lax.ppermute(value, axis, [(k, (k + steps) % count) for k in range(count)])]
    pallas_call x0 -> x9, Pallas kernels: none -> 10.7 us  [the longest x8 9.55 us: call(): pl.pallas_call(body, name=name, out_shape=[jax.ShapeDtypeStruct(s, d) for...]
    dot_general x12 -> x0, matrix products: 5.13 us -> none  [sandwich(): jnp.dot(a, b, precision=lax.Precision.HIGH, preferred_element_type=jnp.fl...]
    unnamed x28 -> x10, local copies, waits for them, and re-layouts: 4.56 us -> 0.02 us
    ppermute x21, starting transfers between devices: 25.8 us -> 30.2 us  [moved(): lax.ppermute(value, axis, [(k, (k + steps) % count) for k in range(count)])]
    slice x9 -> x0, local copies, waits for them, and re-layouts: 4.04 us -> none  [the longest x2 1.93 us: local(): at[0]]
    another operation x5 -> x0, other arithmetic: 1.37 us -> none  [the longest x1 0.66 us: local(): offs = jnp.stack([o[0, 0, 0] for o in off])]
  transfers between devices with their start and end apart: 21 -> 21, of which waited for: 7 -> 9; matrix products, arithmetic and copies ran while one was open for 15% -> 0% of each run, Pallas kernels for 0% -> 13%
where the time goes in v2:
time: 80.9 us; the launch traced here: 80.7 us
  waiting for transfers between devices  37.7 us (47%)
  starting transfers between devices  30.2 us (37%)
  Pallas kernels  10.7 us (13%)
  local copies, waits for them, and re-layouts  1.06 us (1%)
  other arithmetic  0.84 us (1%)
    ppermute x21, waiting for transfers between devices, moved(): lax.ppermute(value, axis, [(k, (k + steps) % count) for k in range(count)])  37.7 us
    ppermute x21, starting transfers between devices, moved(): lax.ppermute(value, axis, [(k, (k + steps) % count) for k in range(count)])  30.2 us
    pallas_call x8, Pallas kernels, call(): pl.pallas_call(body, name=name, out_shape=[jax.ShapeDtypeStruct(s, d) for...  9.55 us
  transfers between devices with their start and end apart: 21, of which 9 were waited for; matrix products, arithmetic and copies ran while one was open for 0% of the time, Pallas kernels for 13%

profile of v2, /device:TPU:0, one launch (start us, length us, event | category | flops | bytes accessed | tf_op | source)
XLA Modules:
  0.0 80.7 jit_solution(16759649812476353317)
XLA Ops:
  0.0 1.0 %slice_bitcast_fusion = (f32[2,128,128]{2,1,0:T(8,128)S(1)}, f32[2,128,128]{2,1,0:T(8,128)S(1)}) fusion(f32[2,2,128,128]{3,2,1,0:T(8,128)} %param.6), kind=kLoop, calls=%fused_computation.6 | loop fusion | bytes 524288 | tf_op jit(solution)/shard_map/squeeze | solution.py:225
  1.0 5.1 %collective-permute-start.13 = (f32[2,128,128]{2,1,0:T(8,128)S(1)}, f32[2,128,128]{2,1,0:T(8,128)S(1)}, u32[]{:S(2)}, u32[]{:S(2)}) collective-permute-start(f32[2,128,128]{2,1,0:T(8,128)S(1)} %get-tuple-element.44.own_ref), channel_id=1, source_target_pairs={{0,3},{1,0},{2,1},{3,2},{4,7},{5,4},{6,5},{7,6},{8,11},{9,8},{10,9... | collective-permute-start | bytes 393224 | tf_op jit(solution)/shard_map/ppermute | solution.py:22
  6.2 0.0 collective-permute-start.6
  6.2 2.8 %collective-permute-done.13.near_ref = f32[2,128,128]{2,1,0:T(8,128)S(1)} collective-permute-done((f32[2,128,128]{2,1,0:T(8,128)S(1)}, f32[2,128,128]{2,1,0:T(8,128)S(1)}, u32[]{:S(2)}, u32[]{:S(2)}) %collective-permute-start.13) | collective-permute-done | bytes 131104 | tf_op jit(solution)/shard_map/ppermute | solution.py:22
  8.9 4.3 %collective-permute-start.14 = (f32[2,128,128]{2,1,0:T(8,128)S(1)}, f32[2,128,128]{2,1,0:T(8,128)S(1)}, u32[]{:S(2)}, u32[]{:S(2)}) collective-permute-start(f32[2,128,128]{2,1,0:T(8,128)S(1)} %collective-permute-done.13.near_ref), channel_id=1, source_target_pairs={{0,3},{1,0},{2,1},{3,2},{4,7},{5,4},{6,5},{7,6},{8,11},{9,8},{10,9... | collective-permute-start | bytes 393224 | tf_op jit(solution)/shard_map/ppermute | solution.py:22
  13.2 1.5 %collective-permute-start.1 = (s32[1,2]{1,0:T(1,128)S(1)}, s32[1,2]{1,0:T(1,128)S(1)}, u32[]{:S(2)}, u32[]{:S(2)}) collective-permute-start(s32[1,2]{1,0:T(1,128)S(1)} %bitcast.17), channel_id=1, source_target_pairs={{0,8},{4,12},{8,16},{12,20},{16,24},{20,28},{24,0},{28,4},{1,9},{5... | collective-permute-start | bytes 32 | tf_op jit(solution)/shard_map/ppermute | solution.py:22
  14.7 2.4 %collective-permute-done.off1 = s32[1,2]{1,0:T(1,128)S(1)} collective-permute-done((s32[1,2]{1,0:T(1,128)S(1)}, s32[1,2]{1,0:T(1,128)S(1)}, u32[]{:S(2)}, u32[]{:S(2)}) %collective-permute-start) | collective-permute-done | bytes 40 | tf_op jit(solution)/shard_map/ppermute | solution.py:22
  17.1 0.6 collective-permute-done.1.off2
  17.7 0.9 %spread.3 = (f32[2,128,256]{2,1,0:T(8,128)S(1)}, f32[2,128,256]{2,1,0:T(8,128)S(1)}, f32[2,128,256]{2,1,0:T(8,128)S(1)}) custom-call(s32[1,2]{1,0:T(1,128)S(1)} %bitcast.18, s32[1,2]{1,0:T(1,128)S(1)} %collective-permute-done.off1, s32[1,2]{1,0:T(1,128)S(1)} %collective-permute-done.1.off2, f32[2,128,128]{2,1,0:T(8,128)S(1)} %get-tuple-element.44.own_ref, ...), custom_call_target="tpu_custom_call" | custom-call | tf_op jit(solution)/shard_map/spread/pallas_call | solution.py:26
  18.6 0.5 collective-permute-start.15
  19.1 2.2 %collective-permute-start.16 = (f32[2,128,256]{2,1,0:T(8,128)S(1)}, f32[2,128,256]{2,1,0:T(8,128)S(1)}, u32[]{:S(2)}, u32[]{:S(2)}) collective-permute-start(f32[2,128,256]{2,1,0:T(8,128)S(1)} %get-tuple-element.34), channel_id=1, source_target_pairs={{0,28},{4,0},{8,4},{12,8},{16,12},{20,16},{24,20},{28,24},{1,29},{... | collective-permute-start | bytes 786440 | tf_op jit(solution)/shard_map/ppermute | solution.py:22
  21.3 2.3 %collective-permute-start.2 = (f32[2,128,128]{2,1,0:T(8,128)S(1)}, f32[2,128,128]{2,1,0:T(8,128)S(1)}, u32[]{:S(2)}, u32[]{:S(2)}) collective-permute-start(f32[2,128,128]{2,1,0:T(8,128)S(1)} %get-tuple-element.43.own_ref), channel_id=1, source_target_pairs={{0,3},{1,0},{2,1},{3,2},{4,7},{5,4},{6,5},{7,6},{8,11},{9,8},{10,9... | collective-permute-start | bytes 393224 | tf_op jit(solution)/shard_map/ppermute | solution.py:22
  23.6 2.7 %collective-permute-done.2.near_ref = f32[2,128,128]{2,1,0:T(8,128)S(1)} collective-permute-done((f32[2,128,128]{2,1,0:T(8,128)S(1)}, f32[2,128,128]{2,1,0:T(8,128)S(1)}, u32[]{:S(2)}, u32[]{:S(2)}) %collective-permute-start.2) | collective-permute-done | bytes 131104 | tf_op jit(solution)/shard_map/ppermute | solution.py:22
  26.3 4.1 %collective-permute-start.3 = (f32[2,128,128]{2,1,0:T(8,128)S(1)}, f32[2,128,128]{2,1,0:T(8,128)S(1)}, u32[]{:S(2)}, u32[]{:S(2)}) collective-permute-start(f32[2,128,128]{2,1,0:T(8,128)S(1)} %collective-permute-done.2.near_ref), channel_id=1, source_target_pairs={{0,3},{1,0},{2,1},{3,2},{4,7},{5,4},{6,5},{7,6},{8,11},{9,8},{10,9... | collective-permute-start | bytes 393224 | tf_op jit(solution)/shard_map/ppermute | solution.py:22
  30.4 0.0 collective-permute-done.6.resid_ref
  30.4 1.1 %back.1.back_ref = f32[2,256,256]{2,1,0:T(8,128)S(1)} custom-call(f32[2,256,256]{2,1,0:T(8,128)S(1)} %collective-permute-done.6.resid_ref, bf16[2,2,256,256]{3,2,1,0:T(8,128)(2,1)S(1)} %copy-done.2), custom_call_target="tpu_custom_call" | custom-call | tf_op jit(solution)/shard_map/back/pallas_call | solution.py:26
  31.5 0.0 collective-permute-done.15.up_ref
  31.6 2.0 %wave.1 = (f32[3,128,256]{2,1,0:T(8,128)S(1)}, f32[3,128,256]{2,1,0:T(8,128)S(1)}, f32[3,128,256]{2,1,0:T(8,128)S(1)}) custom-call(s32[1,2]{1,0:T(1,128)S(1)} %collective-permute-done.off1, f32[2,128,256]{2,1,0:T(8,128)S(1)} %collective-permute-done.15.up_ref, f32[2,128,256]{2,1,0:T(8,128)S(1)} %get-tuple-element.33.mid_ref, ...), custom_call_target="tpu_custom_call" | custom-call | tf_op jit(solution)/shard_map/wave/pallas_call | solution.py:26
  33.6 0.1 collective-permute-start.17
  33.6 0.5 collective-permute-start.18
  34.1 0.0 collective-permute-done.3.far_ref
  34.1 0.9 %spread.2 = (f32[2,128,256]{2,1,0:T(8,128)S(1)}, f32[2,128,256]{2,1,0:T(8,128)S(1)}, f32[2,128,256]{2,1,0:T(8,128)S(1)}) custom-call(s32[1,2]{1,0:T(1,128)S(1)} %bitcast.19, s32[1,2]{1,0:T(1,128)S(1)} %collective-permute-done.off1, s32[1,2]{1,0:T(1,128)S(1)} %collective-permute-done.1.off2, f32[2,128,128]{2,1,0:T(8,128)S(1)} %get-tuple-element.43.own_ref, ...), custom_call_target="tpu_custom_call" | custom-call | tf_op jit(solution)/shard_map/spread/pallas_call | solution.py:26
  35.1 0.6 collective-permute-start.4
  35.7 2.1 %collective-permute-start.5 = (f32[2,128,256]{2,1,0:T(8,128)S(1)}, f32[2,128,256]{2,1,0:T(8,128)S(1)}, u32[]{:S(2)}, u32[]{:S(2)}) collective-permute-start(f32[2,128,256]{2,1,0:T(8,128)S(1)} %get-tuple-element.25), channel_id=1, source_target_pairs={{0,28},{4,0},{8,4},{12,8},{16,12},{20,16},{24,20},{28,24},{1,29},{... | collective-permute-start | bytes 786440 | tf_op jit(solution)/shard_map/ppermute | solution.py:22
  37.8 13.0 %collective-permute-done.4.up_ref = f32[2,128,256]{2,1,0:T(8,128)S(1)} collective-permute-done((f32[2,128,256]{2,1,0:T(8,128)S(1)}, f32[2,128,256]{2,1,0:T(8,128)S(1)}, u32[]{:S(2)}, u32[]{:S(2)}) %collective-permute-start.4) | collective-permute-done | bytes 262176 | tf_op jit(solution)/shard_map/ppermute | solution.py:22
  50.7 0.0 collective-permute-done.5.down_ref
  50.8 1.9 %pull.1 = (f32[2,128,256]{2,1,0:T(8,128)S(1)}, f32[2,128,256]{2,1,0:T(8,128)S(1)}, f32[2,128,256]{2,1,0:T(8,128)S(1)}) custom-call(s32[1,2]{1,0:T(1,128)S(1)} %collective-permute-done.off1, f32[2,128,256]{2,1,0:T(8,128)S(1)} %collective-permute-done.4.up_ref, f32[2,128,256]{2,1,0:T(8,128)S(1)} %get-tuple-element.24.mid_ref, ...), custom_call_target="tpu_custom_call" | custom-call | tf_op jit(solution)/shard_map/pull/pallas_call | solution.py:26
  52.6 0.5 collective-permute-start.7
  53.1 0.1 collective-permute-start.8
  53.2 0.0 collective-permute-done.18.below_ref
  53.2 0.9 %merge.3 = (f32[3,128,128]{2,1,0:T(8,128)S(1)}, f32[3,128,128]{2,1,0:T(8,128)S(1)}, f32[3,128,128]{2,1,0:T(8,128)S(1)}) custom-call(s32[1,2]{1,0:T(1,128)S(1)} %bitcast.20, s32[1,2]{1,0:T(1,128)S(1)} %collective-permute-done.off1, s32[1,2]{1,0:T(1,128)S(1)} %collective-permute-done.1.off2, f32[3,128,256]{2,1,0:T(8,128)S(1)} %collective-permute-done.17.above_ref, ...), custom_call_target="tpu_custom_call" | custom-call | tf_op jit(solution)/shard_map/merge/pallas_call | solution.py:26
  54.1 0.1 collective-permute-start.19
  54.2 1.2 %joined.1.offs0 = s32[3,2]{1,0:T(4,128)S(1)} custom-call(s32[1,2]{1,0:T(1,128)S(1)} %bitcast.21, s32[1,2]{1,0:T(1,128)S(1)} %collective-permute-done.off1, s32[1,2]{1,0:T(1,128)S(1)} %collective-permute-done.1.off2), custom_call_target="tpu_custom_call" | custom-call | tf_op jit(solution)/shard_map/joined/pallas_call | solution.py:243
  55.4 0.1 collective-permute-start.11
  55.5 4.4 %collective-permute-start.12 = (s32[3,2]{1,0:T(4,128)S(1)}, s32[3,2]{1,0:T(4,128)S(1)}, u32[]{:S(2)}, u32[]{:S(2)}) collective-permute-start(s32[3,2]{1,0:T(4,128)S(1)} %joined.1.offs0), channel_id=1, source_target_pairs={{0,2},{1,3},{2,0},{3,1},{4,6},{5,7},{6,4},{7,5},{8,10},{9,11},{10,... | collective-permute-start | bytes 80 | tf_op jit(solution)/shard_map/ppermute | solution.py:22
  59.8 3.2 %collective-permute-done.11.offs1 = s32[3,2]{1,0:T(4,128)S(1)} collective-permute-done((s32[3,2]{1,0:T(4,128)S(1)}, s32[3,2]{1,0:T(4,128)S(1)}, u32[]{:S(2)}, u32[]{:S(2)}) %collective-permute-start.11) | collective-permute-done | bytes 56 | tf_op jit(solution)/shard_map/ppermute | solution.py:22
  63.1 0.0 collective-permute-done.12.offs2
  63.1 0.9 %bright.1 = f32[128,128]{1,0:T(8,128)S(1)} custom-call(s32[3,2]{1,0:T(4,128)S(1)} %joined.1.offs0, s32[3,2]{1,0:T(4,128)S(1)} %collective-permute-done.11.offs1, s32[3,2]{1,0:T(4,128)S(1)} %collective-permute-done.12.offs2, f32[2,256,256]{2,1,0:T(8,128)S(1)} %copy-done), custom_call_target="tpu_custom_call" | custom-call | tf_op jit(solution)/shard_map/bright/pallas_call | solution.py:26
  64.0 0.0 collective-permute-done.8.below_ref
  64.0 0.8 %merge.2 = (f32[2,128,128]{2,1,0:T(8,128)S(1)}, f32[2,128,128]{2,1,0:T(8,128)S(1)}, f32[2,128,128]{2,1,0:T(8,128)S(1)}) custom-call(s32[1,2]{1,0:T(1,128)S(1)} %bitcast.22, s32[1,2]{1,0:T(1,128)S(1)} %collective-permute-done.off1, s32[1,2]{1,0:T(1,128)S(1)} %collective-permute-done.1.off2, f32[2,128,256]{2,1,0:T(8,128)S(1)} %collective-permute-done.7.above_ref, ...), custom_call_target="tpu_custom_call" | custom-call | tf_op jit(solution)/shard_map/merge/pallas_call | solution.py:26
  64.9 0.6 collective-permute-start.9
  65.5 0.0 collective-permute-done.19
  65.6 1.3 %collective-permute-start.20 = (f32[3,128,128]{2,1,0:T(8,128)S(1)}, f32[3,128,128]{2,1,0:T(8,128)S(1)}, u32[]{:S(2)}, u32[]{:S(2)}) collective-permute-start(f32[3,128,128]{2,1,0:T(8,128)S(1)} %add.28), channel_id=1, source_target_pairs={{0,1},{1,2},{2,3},{3,0},{4,5},{5,6},{6,7},{7,4},{8,9},{9,10},{10,1... | collective-permute-start | bytes 589832 | tf_op jit(solution)/shard_map/ppermute | solution.py:22
  66.8 6.3 %collective-permute-done.9 = f32[2,128,128]{2,1,0:T(8,128)S(1)} collective-permute-done((f32[2,128,128]{2,1,0:T(8,128)S(1)}, f32[2,128,128]{2,1,0:T(8,128)S(1)}, u32[]{:S(2)}, u32[]{:S(2)}) %collective-permute-start.9) | collective-permute-done | bytes 131104 | tf_op jit(solution)/shard_map/ppermute | solution.py:22
  73.1 0.1 collective-permute-start.10
  73.2 3.7 %collective-permute-done.20 = f32[3,128,128]{2,1,0:T(8,128)S(1)} collective-permute-done((f32[3,128,128]{2,1,0:T(8,128)S(1)}, f32[3,128,128]{2,1,0:T(8,128)S(1)}, u32[]{:S(2)}, u32[]{:S(2)}) %collective-permute-start.20) | collective-permute-done | bytes 196640 | tf_op jit(solution)/shard_map/ppermute | solution.py:22
  77.0 3.0 %collective-permute-done.10 = f32[2,128,128]{2,1,0:T(8,128)S(1)} collective-permute-done((f32[2,128,128]{2,1,0:T(8,128)S(1)}, f32[2,128,128]{2,1,0:T(8,128)S(1)}, u32[]{:S(2)}, u32[]{:S(2)}) %collective-permute-start.10) | collective-permute-done | bytes 131104 | tf_op jit(solution)/shard_map/ppermute | solution.py:22
  80.0 0.7 pad_maximum_fusion
  (21 shorter events, 0.1 us)
Async XLA Ops:
  0.0 30.4 %copy-start.2 = (bf16[2,2,256,256]{3,2,1,0:T(8,128)(2,1)S(1)}, bf16[2,2,256,256]{3,2,1,0:T(8,128)(2,1)}, u32[]{:S(2)}) copy-start(bf16[2,2,256,256]{3,2,1,0:T(8,128)(2,1)} %constant.3.clone.mat_ref) | copy-start | bytes 1572868
  1.0 7.9 %collective-permute-start.13 = (f32[2,128,128]{2,1,0:T(8,128)S(1)}, f32[2,128,128]{2,1,0:T(8,128)S(1)}, u32[]{:S(2)}, u32[]{:S(2)}) collective-permute-start(f32[2,128,128]{2,1,0:T(8,128)S(1)} %get-tuple-element.44.own_ref), channel_id=1, source_target_pairs={{0,3},{1,0},{2,1},{3,2},{4,7},{5,4},{6,5},{7,6},{8,11},{9,8},{10,9... | collective-permute-start | bytes 393224 | tf_op jit(solution)/shard_map/ppermute | solution.py:22
  6.2 7.0 %copy-start.3 = (s32[1,1,1,2]{3,2,1,0:T(1,128)S(1)}, s32[1,1,1,2]{3,2,1,0:T(1,128)}, u32[]{:S(2)}) copy-start(s32[1,1,1,2]{3,2,1,0:T(1,128)} %param.8) | copy-start | bytes 28
  6.2 24.2 %collective-permute-start.6 = (f32[2,256,256]{2,1,0:T(8,128)}, f32[2,256,256]{2,1,0:T(8,128)S(1)}, u32[]{:S(2)}, u32[]{:S(2)}) collective-permute-start(f32[2,256,256]{2,1,0:T(8,128)} %bitcast.23), channel_id=1, source_target_pairs={{0,4},{4,8},{8,12},{12,16},{16,20},{20,24},{24,28},{28,0},{1,5},{5... | collective-permute-start | bytes 1572872 | tf_op jit(solution)/shard_map/ppermute | solution.py:22
  8.9 8.8 %collective-permute-start.14 = (f32[2,128,128]{2,1,0:T(8,128)S(1)}, f32[2,128,128]{2,1,0:T(8,128)S(1)}, u32[]{:S(2)}, u32[]{:S(2)}) collective-permute-start(f32[2,128,128]{2,1,0:T(8,128)S(1)} %collective-permute-done.13.near_ref), channel_id=1, source_target_pairs={{0,3},{1,0},{2,1},{3,2},{4,7},{5,4},{6,5},{7,6},{8,11},{9,8},{10,9... | collective-permute-start | bytes 393224 | tf_op jit(solution)/shard_map/ppermute | solution.py:22
  13.2 3.9 %collective-permute-start = (s32[1,2]{1,0:T(1,128)S(1)}, s32[1,2]{1,0:T(1,128)S(1)}, u32[]{:S(2)}, u32[]{:S(2)}) collective-permute-start(s32[1,2]{1,0:T(1,128)S(1)} %bitcast.16), channel_id=1, source_target_pairs={{0,4},{4,8},{8,12},{12,16},{16,20},{20,24},{24,28},{28,0},{1,5},{5... | collective-permute-start | bytes 32 | tf_op jit(solution)/shard_map/ppermute | solution.py:22
  13.2 4.5 %collective-permute-start.1 = (s32[1,2]{1,0:T(1,128)S(1)}, s32[1,2]{1,0:T(1,128)S(1)}, u32[]{:S(2)}, u32[]{:S(2)}) collective-permute-start(s32[1,2]{1,0:T(1,128)S(1)} %bitcast.17), channel_id=1, source_target_pairs={{0,8},{4,12},{8,16},{12,20},{16,24},{20,28},{24,0},{28,4},{1,9},{5... | collective-permute-start | bytes 32 | tf_op jit(solution)/shard_map/ppermute | solution.py:22
  18.6 12.9 %collective-permute-start.15 = (f32[2,128,256]{2,1,0:T(8,128)S(1)}, f32[2,128,256]{2,1,0:T(8,128)S(1)}, u32[]{:S(2)}, u32[]{:S(2)}) collective-permute-start(f32[2,128,256]{2,1,0:T(8,128)S(1)} %get-tuple-element.32), channel_id=1, source_target_pairs={{0,4},{4,8},{8,12},{12,16},{16,20},{20,24},{24,28},{28,0},{1,5},{5... | collective-permute-start | bytes 786440 | tf_op jit(solution)/shard_map/ppermute | solution.py:22
  19.1 12.4 %collective-permute-start.16 = (f32[2,128,256]{2,1,0:T(8,128)S(1)}, f32[2,128,256]{2,1,0:T(8,128)S(1)}, u32[]{:S(2)}, u32[]{:S(2)}) collective-permute-start(f32[2,128,256]{2,1,0:T(8,128)S(1)} %get-tuple-element.34), channel_id=1, source_target_pairs={{0,28},{4,0},{8,4},{12,8},{16,12},{20,16},{24,20},{28,24},{1,29},{... | collective-permute-start | bytes 786440 | tf_op jit(solution)/shard_map/ppermute | solution.py:22
  21.3 10.2 %copy-start = (f32[2,256,256]{2,1,0:T(8,128)S(1)}, f32[2,256,256]{2,1,0:T(8,128)}, u32[]{:S(2)}) copy-start(f32[2,256,256]{2,1,0:T(8,128)} %probe_ref.5) | copy-start | bytes 1572868
  21.3 10.2 %copy-start.1 = (bf16[2,2,256,256]{3,2,1,0:T(8,128)(2,1)S(1)}, bf16[2,2,256,256]{3,2,1,0:T(8,128)(2,1)}, u32[]{:S(2)}) copy-start(bf16[2,2,256,256]{3,2,1,0:T(8,128)(2,1)} %constant.10.clone.mat_ref) | copy-start | bytes 1572868
  21.3 5.0 %collective-permute-start.2 = (f32[2,128,128]{2,1,0:T(8,128)S(1)}, f32[2,128,128]{2,1,0:T(8,128)S(1)}, u32[]{:S(2)}, u32[]{:S(2)}) collective-permute-start(f32[2,128,128]{2,1,0:T(8,128)S(1)} %get-tuple-element.43.own_ref), channel_id=1, source_target_pairs={{0,3},{1,0},{2,1},{3,2},{4,7},{5,4},{6,5},{7,6},{8,11},{9,8},{10,9... | collective-permute-start | bytes 393224 | tf_op jit(solution)/shard_map/ppermute | solution.py:22
  26.3 7.8 %collective-permute-start.3 = (f32[2,128,128]{2,1,0:T(8,128)S(1)}, f32[2,128,128]{2,1,0:T(8,128)S(1)}, u32[]{:S(2)}, u32[]{:S(2)}) collective-permute-start(f32[2,128,128]{2,1,0:T(8,128)S(1)} %collective-permute-done.2.near_ref), channel_id=1, source_target_pairs={{0,3},{1,0},{2,1},{3,2},{4,7},{5,4},{6,5},{7,6},{8,11},{9,8},{10,9... | collective-permute-start | bytes 393224 | tf_op jit(solution)/shard_map/ppermute | solution.py:22
  33.6 19.6 %collective-permute-start.17 = (f32[3,128,256]{2,1,0:T(8,128)S(1)}, f32[3,128,256]{2,1,0:T(8,128)S(1)}, u32[]{:S(2)}, u32[]{:S(2)}) collective-permute-start(f32[3,128,256]{2,1,0:T(8,128)S(1)} %get-tuple-element.35), channel_id=1, source_target_pairs={{0,28},{4,0},{8,4},{12,8},{16,12},{20,16},{24,20},{28,24},{1,29},{... | collective-permute-start | bytes 1179656 | tf_op jit(solution)/shard_map/ppermute | solution.py:22
  33.6 19.6 %collective-permute-start.18 = (f32[3,128,256]{2,1,0:T(8,128)S(1)}, f32[3,128,256]{2,1,0:T(8,128)S(1)}, u32[]{:S(2)}, u32[]{:S(2)}) collective-permute-start(f32[3,128,256]{2,1,0:T(8,128)S(1)} %get-tuple-element.37), channel_id=1, source_target_pairs={{0,4},{4,8},{8,12},{12,16},{16,20},{20,24},{24,28},{28,0},{1,5},{5... | collective-permute-start | bytes 1179656 | tf_op jit(solution)/shard_map/ppermute | solution.py:22
  35.1 15.7 %collective-permute-start.4 = (f32[2,128,256]{2,1,0:T(8,128)S(1)}, f32[2,128,256]{2,1,0:T(8,128)S(1)}, u32[]{:S(2)}, u32[]{:S(2)}) collective-permute-start(f32[2,128,256]{2,1,0:T(8,128)S(1)} %get-tuple-element.23), channel_id=1, source_target_pairs={{0,4},{4,8},{8,12},{12,16},{16,20},{20,24},{24,28},{28,0},{1,5},{5... | collective-permute-start | bytes 786440 | tf_op jit(solution)/shard_map/ppermute | solution.py:22
  35.7 15.1 %collective-permute-start.5 = (f32[2,128,256]{2,1,0:T(8,128)S(1)}, f32[2,128,256]{2,1,0:T(8,128)S(1)}, u32[]{:S(2)}, u32[]{:S(2)}) collective-permute-start(f32[2,128,256]{2,1,0:T(8,128)S(1)} %get-tuple-element.25), channel_id=1, source_target_pairs={{0,28},{4,0},{8,4},{12,8},{16,12},{20,16},{24,20},{28,24},{1,29},{... | collective-permute-start | bytes 786440 | tf_op jit(solution)/shard_map/ppermute | solution.py:22
  52.6 11.4 %collective-permute-start.7 = (f32[2,128,256]{2,1,0:T(8,128)S(1)}, f32[2,128,256]{2,1,0:T(8,128)S(1)}, u32[]{:S(2)}, u32[]{:S(2)}) collective-permute-start(f32[2,128,256]{2,1,0:T(8,128)S(1)} %get-tuple-element.26), channel_id=1, source_target_pairs={{0,28},{4,0},{8,4},{12,8},{16,12},{20,16},{24,20},{28,24},{1,29},{... | collective-permute-start | bytes 786440 | tf_op jit(solution)/shard_map/ppermute | solution.py:22
  53.1 10.9 %collective-permute-start.8 = (f32[2,128,256]{2,1,0:T(8,128)S(1)}, f32[2,128,256]{2,1,0:T(8,128)S(1)}, u32[]{:S(2)}, u32[]{:S(2)}) collective-permute-start(f32[2,128,256]{2,1,0:T(8,128)S(1)} %get-tuple-element.28), channel_id=1, source_target_pairs={{0,4},{4,8},{8,12},{12,16},{16,20},{20,24},{24,28},{28,0},{1,5},{5... | collective-permute-start | bytes 786440 | tf_op jit(solution)/shard_map/ppermute | solution.py:22
  54.1 11.4 %collective-permute-start.19 = (f32[3,128,128]{2,1,0:T(8,128)S(1)}, f32[3,128,128]{2,1,0:T(8,128)S(1)}, u32[]{:S(2)}, u32[]{:S(2)}) collective-permute-start(f32[3,128,128]{2,1,0:T(8,128)S(1)} %get-tuple-element.40), channel_id=1, source_target_pairs={{0,1},{1,2},{2,3},{3,0},{4,5},{5,6},{6,7},{7,4},{8,9},{9,10},{10,1... | collective-permute-start | bytes 589832 | tf_op jit(solution)/shard_map/ppermute | solution.py:22
  55.4 7.7 %collective-permute-start.11 = (s32[3,2]{1,0:T(4,128)S(1)}, s32[3,2]{1,0:T(4,128)S(1)}, u32[]{:S(2)}, u32[]{:S(2)}) collective-permute-start(s32[3,2]{1,0:T(4,128)S(1)} %joined.1.offs0), channel_id=1, source_target_pairs={{0,1},{1,2},{2,3},{3,0},{4,5},{5,6},{6,7},{7,4},{8,9},{9,10},{10,1... | collective-permute-start | bytes 80 | tf_op jit(solution)/shard_map/ppermute | solution.py:22
  55.5 7.6 %collective-permute-start.12 = (s32[3,2]{1,0:T(4,128)S(1)}, s32[3,2]{1,0:T(4,128)S(1)}, u32[]{:S(2)}, u32[]{:S(2)}) collective-permute-start(s32[3,2]{1,0:T(4,128)S(1)} %joined.1.offs0), channel_id=1, source_target_pairs={{0,2},{1,3},{2,0},{3,1},{4,6},{5,7},{6,4},{7,5},{8,10},{9,11},{10,... | collective-permute-start | bytes 80 | tf_op jit(solution)/shard_map/ppermute | solution.py:22
  64.9 8.2 %collective-permute-start.9 = (f32[2,128,128]{2,1,0:T(8,128)S(1)}, f32[2,128,128]{2,1,0:T(8,128)S(1)}, u32[]{:S(2)}, u32[]{:S(2)}) collective-permute-start(f32[2,128,128]{2,1,0:T(8,128)S(1)} %get-tuple-element.31), channel_id=1, source_target_pairs={{0,1},{1,2},{2,3},{3,0},{4,5},{5,6},{6,7},{7,4},{8,9},{9,10},{10,1... | collective-permute-start | bytes 393224 | tf_op jit(solution)/shard_map/ppermute | solution.py:22
  65.6 11.4 %collective-permute-start.20 = (f32[3,128,128]{2,1,0:T(8,128)S(1)}, f32[3,128,128]{2,1,0:T(8,128)S(1)}, u32[]{:S(2)}, u32[]{:S(2)}) collective-permute-start(f32[3,128,128]{2,1,0:T(8,128)S(1)} %add.28), channel_id=1, source_target_pairs={{0,1},{1,2},{2,3},{3,0},{4,5},{5,6},{6,7},{7,4},{8,9},{9,10},{10,1... | collective-permute-start | bytes 589832 | tf_op jit(solution)/shard_map/ppermute | solution.py:22
  73.1 6.8 %collective-permute-start.10 = (f32[2,128,128]{2,1,0:T(8,128)S(1)}, f32[2,128,128]{2,1,0:T(8,128)S(1)}, u32[]{:S(2)}, u32[]{:S(2)}) collective-permute-start(f32[2,128,128]{2,1,0:T(8,128)S(1)} %add.24), channel_id=1, source_target_pairs={{0,1},{1,2},{2,3},{3,0},{4,5},{5,6},{6,7},{7,4},{8,9},{9,10},{10,1... | collective-permute-start | bytes 393224 | tf_op jit(solution)/shard_map/ppermute | solution.py:22
  76.9 3.0 %copy-start.4 = (f32[2,2,128,128]{3,2,1,0:T(8,128)S(1)}, f32[2,2,128,128]{3,2,1,0:T(8,128)}, u32[]{:S(2)}) copy-start(f32[2,2,128,128]{3,2,1,0:T(8,128)} %param.6) | copy-start | bytes 786436
